TPU v7x, 8 devices: a whole 2x2x1 slice. The times are simulated.
8 devices in a mesh: dp: 1 (over z), tp: 2 (over y), ctx: 4 (over x, core).
Axes of the slice: x: 2, y: 2, z: 1, core: 2. Of those that a mesh axis runs over, the one named last changes fastest.
Arguments:
- x_tokens: bfloat16 [1024, 6144], P(('dp', 'ctx'))
- positions: int32 [1024], P(('dp', 'ctx'))
- w_dq: bfloat16 [6144, 1536], replicated
- g_q: bfloat16 [1536], replicated
- w_uq: bfloat16 [1536, 8192], P(None, 'tp')
- w_qr: bfloat16 [1536, 4096], P(None, 'tp')
- w_dkv: bfloat16 [6144, 512], replicated
- g_kv: bfloat16 [512], replicated
- w_kr: bfloat16 [6144, 64], replicated
- w_uk: bfloat16 [512, 8192], P(None, 'tp')
- w_uv: bfloat16 [512, 8192], P(None, 'tp')
- w_o: bfloat16 [8192, 6144], P('tp')
Outputs:
- output: bfloat16 [1024, 6144], P(('dp', 'ctx'))
All inputs are finite; a program needn't handle non-finite values.
Results may differ from a plain program's by a relative error of at most 0.00851886.
Values are sent between devices in bfloat16 or wider.
A program may use at most 1 GiB of HBM per device.

v0:
```python
import jax
import jax.numpy as jnp
from jax import lax
from jax.sharding import PartitionSpec as P

ROPE_BASE = 10000.0
NORM_EPS = 1e-6
NEG_BIG = -1e30


def rms_norm(act_in, gain_vec):
    inv_rms = lax.rsqrt(jnp.mean(act_in * act_in, axis=-1, keepdims=True) + NORM_EPS)
    return act_in * inv_rms * gain_vec.astype(jnp.float32)


def rope_tables(pos_vals, rope_dim):
    half_dim = rope_dim // 2
    inv_freq = ROPE_BASE ** (-jnp.arange(half_dim, dtype=jnp.float32) * 2.0 / rope_dim)
    angles = pos_vals.astype(jnp.float32)[..., None] * inv_freq
    return jnp.cos(angles), jnp.sin(angles)


def apply_rope(act_in, cos_t, sin_t):
    half_dim = act_in.shape[-1] // 2
    first_half = act_in[..., :half_dim]
    second_half = act_in[..., half_dim:]
    return jnp.concatenate([first_half * cos_t - second_half * sin_t, second_half * cos_t + first_half * sin_t], axis=-1)


def project_tokens(tok_x, tok_pos, w_dq, g_q, w_uq, w_qr, w_dkv, g_kv, w_kr, heads_loc):
    rope_dim = w_kr.shape[1]
    tok_count = tok_x.shape[0]
    cos_t, sin_t = rope_tables(tok_pos, rope_dim)
    c_q = rms_norm(jnp.dot(tok_x, w_dq, preferred_element_type=jnp.float32), g_q).astype(jnp.bfloat16)
    q_nope = jnp.dot(c_q, w_uq, preferred_element_type=jnp.float32).astype(jnp.bfloat16).reshape(tok_count, heads_loc, -1)
    q_rot = jnp.dot(c_q, w_qr, preferred_element_type=jnp.float32).reshape(tok_count, heads_loc, rope_dim)
    q_pe = apply_rope(q_rot, cos_t[:, None, :], sin_t[:, None, :]).astype(jnp.bfloat16)
    c_kv = rms_norm(jnp.dot(tok_x, w_dkv, preferred_element_type=jnp.float32), g_kv).astype(jnp.bfloat16)
    k_pe = apply_rope(jnp.dot(tok_x, w_kr, preferred_element_type=jnp.float32), cos_t, sin_t).astype(jnp.bfloat16)
    return q_nope, q_pe, c_kv, k_pe


def up_project(lat_rows, w_uk, w_uv, heads_loc):
    row_count = lat_rows.shape[0]
    k_nope = jnp.dot(lat_rows, w_uk, preferred_element_type=jnp.float32).astype(jnp.bfloat16).reshape(row_count, heads_loc, -1)
    v_rows = jnp.dot(lat_rows, w_uv, preferred_element_type=jnp.float32).astype(jnp.bfloat16).reshape(row_count, heads_loc, -1)
    return k_nope, v_rows


def block_scores(q_nope, q_pe, k_nope, k_pe, score_scale):
    nope_part = jnp.einsum('qhn,khn->hqk', q_nope, k_nope, preferred_element_type=jnp.float32)
    rope_part = jnp.einsum('qhr,kr->hqk', q_pe, k_pe, preferred_element_type=jnp.float32)
    return (nope_part + rope_part) * score_scale


def block_stats(scores, v_rows):
    blk_max = jnp.max(scores, axis=-1)
    prob_tile = jnp.exp(scores - blk_max[..., None])
    blk_sum = jnp.sum(prob_tile, axis=-1)
    blk_acc = jnp.einsum('hqk,khv->hqv', prob_tile.astype(jnp.bfloat16), v_rows, preferred_element_type=jnp.float32)
    return blk_max, blk_sum, blk_acc


def merge_stats(run_state, update):
    old_max, old_sum, old_acc = run_state
    new_max, new_sum, new_acc = update
    top_max = jnp.maximum(old_max, new_max)
    old_w = jnp.exp(old_max - top_max)
    new_w = jnp.exp(new_max - top_max)
    return top_max, old_sum * old_w + new_sum * new_w, old_acc * old_w[..., None] + new_acc * new_w[..., None]


def solution(mesh):
    ctx_count = mesh.shape['ctx']
    next_perm = [(src, (src + 1) % ctx_count) for src in range(ctx_count)]
    tok_spec = P(('dp', 'ctx'), None)
    pos_spec = P(('dp', 'ctx'))
    full_mat = P(None, None)
    full_vec = P(None)
    col_spec = P(None, 'tp')
    row_spec = P('tp', None)

    def local_step(tok_x, tok_pos, w_dq, g_q, w_uq, w_qr, w_dkv, g_kv, w_kr, w_uk, w_uv, w_o):
        my_index = lax.axis_index('ctx')
        half_len = tok_x.shape[0] // 2
        rope_dim = w_kr.shape[1]
        heads_loc = w_qr.shape[1] // rope_dim
        nope_dim = w_uq.shape[1] // heads_loc
        value_dim = w_uv.shape[1] // heads_loc
        score_scale = (nope_dim + rope_dim) ** -0.5
        q_nope, q_pe, c_kv, k_pe = project_tokens(tok_x, tok_pos, w_dq, g_q, w_uq, w_qr, w_dkv, g_kv, w_kr, heads_loc)
        k_nope, v_rows = up_project(c_kv, w_uk, w_uv, heads_loc)
        scores = block_scores(q_nope, q_pe, k_nope, k_pe, score_scale)
        visible = tok_pos[None, :] <= tok_pos[:, None]
        run_state = block_stats(jnp.where(visible[None], scores, NEG_BIG), v_rows)

        def attend_lower(lat_blk, rot_blk, run_state):
            k_low, v_low = up_project(lat_blk[:half_len], w_uk, w_uv, heads_loc)
            update = block_stats(block_scores(q_nope, q_pe, k_low, rot_blk[:half_len], score_scale), v_low)
            return merge_stats(run_state, update)

        def attend_upper(lat_blk, rot_blk, run_state):
            k_both, v_both = up_project(lat_blk, w_uk, w_uv, heads_loc)
            update = block_stats(block_scores(q_nope[half_len:], q_pe[half_len:], k_both, rot_blk, score_scale), v_both)
            old_max, old_sum, old_acc = run_state
            top_max, top_sum, top_acc = merge_stats((old_max[:, half_len:], old_sum[:, half_len:], old_acc[:, half_len:]), update)
            return (jnp.concatenate([old_max[:, :half_len], top_max], axis=1),
                    jnp.concatenate([old_sum[:, :half_len], top_sum], axis=1),
                    jnp.concatenate([old_acc[:, :half_len], top_acc], axis=1))

        def ctx_step(hop_idx, loop_carry):
            lat_blk, rot_blk, run_state = loop_carry
            lat_blk = lax.ppermute(lat_blk, 'ctx', next_perm)
            rot_blk = lax.ppermute(rot_blk, 'ctx', next_perm)
            src_index = (my_index - hop_idx) % ctx_count
            run_state = lax.cond(src_index < my_index, attend_lower, attend_upper, lat_blk, rot_blk, run_state)
            return lat_blk, rot_blk, run_state

        loop_carry = lax.fori_loop(1, ctx_count, ctx_step, (c_kv, k_pe, run_state))
        run_max, run_sum, run_acc = loop_carry[2]
        attn_out = (run_acc / run_sum[..., None]).astype(jnp.bfloat16)
        y_part = jnp.einsum('htv,hvd->td', attn_out, w_o.reshape(heads_loc, value_dim, -1), preferred_element_type=jnp.float32)
        return lax.psum(y_part, 'tp').astype(jnp.bfloat16)

    return jax.shard_map(local_step, mesh=mesh,
                         in_specs=(tok_spec, pos_spec, full_mat, full_vec, col_spec, col_spec, full_mat, full_vec, full_mat, col_spec, col_spec, row_spec),
                         out_specs=tok_spec, check_vma=False)
```

profile of v0, /device:TPU:0, one launch (start us, length us, event | category | flops | bytes accessed | tf_op | source)
XLA Modules:
  0.0 277.9 jit_solution(12693809014680956844)
XLA Ops:
  0.0 1.9 copy-done
  1.9 9.1 %multiply_reduce_fusion = (f32[256]{0:T(256)S(1)}, f32[256,1536]{1,0:T(8,128)S(1)}) fusion(bf16[256,6144]{1,0:T(8,128)(2,1)S(1)} %copy-done, bf16[6144,1536]{1,0:T(8,128)(2,1)} %param.18), kind=kOutput, calls=%fused_computation.74 | convolution fusion | flops 4832624640 | bytes 23593984 | tf_op jit(solution)/shard_map/dot_general | solution.py:34
  11.0 5.7 %fusion.53 = f32[256,2048]{0,1:T(8,128)S(1)} fusion(bf16[1536,2048]{1,0:T(8,128)(2,1)} %param.21, f32[256,1536]{1,0:T(8,128)S(1)} %get-tuple-element.416, f32[1536]{0:T(1024)S(1)} %convert_element_type.66, f32[256]{0:T(256)S(1)} %add_rsqrt_fusion), kind=kOutput, calls=%fused_computation.90 | convolution fusion | flops 1611792384 | bytes 9968640 | tf_op jit(solution)/shard_map/dot_general | solution.py:36
  18.5 4.1 %fusion.49 = bf16[32,32,8,128]{3,2,1,0:T(8,128)(2,1)S(1)} fusion(bf16[1536,4096]{1,0:T(8,128)(2,1)S(1)} %copy-done.13, f32[256,1536]{1,0:T(8,128)S(1)} %get-tuple-element.416, f32[1536]{0:T(1024)S(1)} %convert_element_type.66, f32[256]{0:T(256)S(1)} %add_rsqrt_fusion), kind=kOutput, calls=%fused_computation.70 | convolution fusion | flops 3223453696 | bytes 16260096 | tf_op jit(solution)/shard_map/dot_general | solution.py:35
  22.7 1.9 multiply_reduce_fusion.1
  27.5 2.0 fusion.56
  31.0 3.8 %fusion.40 = f32[32,256,128]{2,1,0:T(8,128)} fusion(f32[32,256,256]{1,2,0:T(8,128)S(1)} %get-tuple-element.418, f32[32,256]{1,0:T(8,128)S(1)} %get-tuple-element.501, bf16[32,32,8,128]{3,2,1,0:T(8,128)(2,1)S(1)} %fusion.51), kind=kOutput, calls=%fused_computation.60 | convolution fusion | flops 541065216 | bytes 14712832 | tf_op jit(solution)/shard_map/hqk,khv->hqv/dot_general | solution.py:60
  36.6 1.9 copy.81
  38.5 67.6 %while.23 = (s32[]{:T(128)}, bf16[256,512]{1,0:T(8,128)(2,1)S(1)}, bf16[256,64]{0,1:T(8,128)(2,1)S(1)}, f32[32,256]{1,0:T(8,128)S(1)}, f32[32,256]{1,0:T(8,128)S...) while((s32[]{:T(128)}, bf16[256,512]{1,0:T(8,128)(2,1)S(1)}, ...), condition=%wide.region_11.12_spmd, body=%wide.region_4.11_spmd.sunk | while | flops 2830663680 | bytes 97927776 | solution.py:119
  39.3 2.6 collective-permute-start.1
  41.9 3.7 %collective-permute-done.1 = bf16[256,64]{0,1:T(8,128)(2,1)S(1)} collective-permute-done((bf16[256,64]{0,1:T(8,128)(2,1)S(1)}, bf16[256,64]{0,1:T(8,128)(2,1)S(1)}, u32[]{:S(2)}, u32[]{:S(2)}) %collective-permute-start.1) | collective-permute-done | bytes 32800 | tf_op jit(solution)/shard_map/while/body/eval_jaxpr/ppermute | solution.py:114
  45.7 16.0 %conditional.2 = (f32[32,256]{1,0:T(8,128)S(1)}, f32[32,256]{1,0:T(8,128)S(1)}, f32[32,256,128]{2,1,0:T(8,128)}) conditional(s32[]{:T(128)} %convert_element_type.110, (f32[32,256]{1,0:T(8,128)S(1)}, bf16[256,512]{1,0:T(8,128)(2,1)S(1)}, bf16[512,4096]{1,0:T(8,128)(2,1)}, bf16[256,32,128]{2,0,1:T(8,128)(2,1)}, bf16[256,32,64]{0,2,1:T(8,128)(2,1)S(1)}, ...), branch_computations={%region_5.7_spmd, %region_8.10_spmd} | conditional | flops 2830663680 | bytes 96157808 | solution.py:116
  45.7 3.5 %fusion.10 = bf16[32,32,8,128]{3,2,1,0:T(8,128)(2,1)S(1)} fusion(bf16[256,512]{1,0:T(8,128)(2,1)S(1)} %get-tuple-element.309, bf16[512,4096]{1,0:T(8,128)(2,1)} %get-tuple-element.310), kind=kOutput, calls=%fused_computation.15 | convolution fusion | flops 1074790400 | bytes 6553600 | tf_op jit(solution)/shard_map/while/body/eval_jaxpr/cond/branch_0_fun/dot_general | solution.py:45
  49.9 2.0 fusion.54
  56.3 2.7 multiply_add_fusion
  59.3 2.4 pad_maximum_fusion
  61.9 2.5 collective-permute-start.1
  64.4 3.5 %collective-permute-done.1 = bf16[256,64]{0,1:T(8,128)(2,1)S(1)} collective-permute-done((bf16[256,64]{0,1:T(8,128)(2,1)S(1)}, bf16[256,64]{0,1:T(8,128)(2,1)S(1)}, u32[]{:S(2)}, u32[]{:S(2)}) %collective-permute-start.1) | collective-permute-done | bytes 32800 | tf_op jit(solution)/shard_map/while/body/eval_jaxpr/ppermute | solution.py:114
  67.9 16.0 %conditional.2 = (f32[32,256]{1,0:T(8,128)S(1)}, f32[32,256]{1,0:T(8,128)S(1)}, f32[32,256,128]{2,1,0:T(8,128)}) conditional(s32[]{:T(128)} %convert_element_type.110, (f32[32,256]{1,0:T(8,128)S(1)}, bf16[256,512]{1,0:T(8,128)(2,1)S(1)}, bf16[512,4096]{1,0:T(8,128)(2,1)}, bf16[256,32,128]{2,0,1:T(8,128)(2,1)}, bf16[256,32,64]{0,2,1:T(8,128)(2,1)S(1)}, ...), branch_computations={%region_5.7_spmd, %region_8.10_spmd} | conditional | flops 2830663680 | bytes 96157808 | solution.py:116
  67.9 3.5 %fusion.10 = bf16[32,32,8,128]{3,2,1,0:T(8,128)(2,1)S(1)} fusion(bf16[256,512]{1,0:T(8,128)(2,1)S(1)} %get-tuple-element.309, bf16[512,4096]{1,0:T(8,128)(2,1)} %get-tuple-element.310), kind=kOutput, calls=%fused_computation.15 | convolution fusion | flops 1074790400 | bytes 6553600 | tf_op jit(solution)/shard_map/while/body/eval_jaxpr/cond/branch_0_fun/dot_general | solution.py:45
  72.1 2.0 fusion.54
  78.5 2.7 multiply_add_fusion
  81.5 2.4 pad_maximum_fusion
  84.1 2.7 collective-permute-start.1
  86.8 3.3 %collective-permute-done.1 = bf16[256,64]{0,1:T(8,128)(2,1)S(1)} collective-permute-done((bf16[256,64]{0,1:T(8,128)(2,1)S(1)}, bf16[256,64]{0,1:T(8,128)(2,1)S(1)}, u32[]{:S(2)}, u32[]{:S(2)}) %collective-permute-start.1) | collective-permute-done | bytes 32800 | tf_op jit(solution)/shard_map/while/body/eval_jaxpr/ppermute | solution.py:114
  90.1 16.0 %conditional.2 = (f32[32,256]{1,0:T(8,128)S(1)}, f32[32,256]{1,0:T(8,128)S(1)}, f32[32,256,128]{2,1,0:T(8,128)}) conditional(s32[]{:T(128)} %convert_element_type.110, (f32[32,256]{1,0:T(8,128)S(1)}, bf16[256,512]{1,0:T(8,128)(2,1)S(1)}, bf16[512,4096]{1,0:T(8,128)(2,1)}, bf16[256,32,128]{2,0,1:T(8,128)(2,1)}, bf16[256,32,64]{0,2,1:T(8,128)(2,1)S(1)}, ...), branch_computations={%region_5.7_spmd, %region_8.10_spmd} | conditional | flops 2830663680 | bytes 96157808 | solution.py:116
  90.1 3.5 %fusion.10 = bf16[32,32,8,128]{3,2,1,0:T(8,128)(2,1)S(1)} fusion(bf16[256,512]{1,0:T(8,128)(2,1)S(1)} %get-tuple-element.309, bf16[512,4096]{1,0:T(8,128)(2,1)} %get-tuple-element.310), kind=kOutput, calls=%fused_computation.15 | convolution fusion | flops 1074790400 | bytes 6553600 | tf_op jit(solution)/shard_map/while/body/eval_jaxpr/cond/branch_0_fun/dot_general | solution.py:45
  94.3 2.0 fusion.54
  100.7 2.7 multiply_add_fusion
  103.7 2.4 pad_maximum_fusion
  106.1 23.7 %convolution_bitcast_fusion = f32[256,6144]{1,0:T(8,128)} fusion(bf16[32,128,6144]{2,1,0:T(8,128)(2,1)} %bitcast.97, f32[32,256,128]{2,1,0:T(8,128)} %get-tuple-element.343, f32[32,256]{1,0:T(8,128)S(1)} %get-tuple-element.344), kind=kOutput, calls=%fused_computation.54 | convolution fusion | flops 12886999040 | bytes 60850176 | tf_op jit(solution)/shard_map/htv,hvd->td/dot_general | solution.py:122
  129.8 148.1 %all-reduce.1 = bf16[256,6144]{1,0:T(8,128)(2,1)} all-reduce(f32[256,6144]{1,0:T(8,128)} %convolution_bitcast_fusion), channel_id=1, replica_groups=mesh['dp'=1,'tp'=2,'ctx'=4] {'tp'}, use_global_device_ids=true, to_apply=%region_12.13 | all-reduce | flops 1572864 | bytes 9437184 | tf_op jit(solution)/shard_map/psum | solution.py:123
  (81 shorter events, 25.1 us)
Async XLA Ops:
  0.0 1.9 copy-start
  0.0 11.0 %copy-start.11 = (bf16[1536]{0:T(1024)(128)(2,1)S(1)}, bf16[1536]{0:T(1024)(128)(2,1)}, u32[]{:S(2)}) copy-start(bf16[1536]{0:T(1024)(128)(2,1)} %param.19) | copy-start | bytes 9220
  11.0 5.8 %copy-start.9 = (bf16[6144,64]{0,1:T(8,128)(2,1)S(1)}, bf16[6144,64]{0,1:T(8,128)(2,1)}, u32[]{:S(2)}) copy-start(bf16[6144,64]{0,1:T(8,128)(2,1)} %param.24) | copy-start | bytes 2359300
  11.0 6.9 %copy-start.10 = (s32[256]{0:T(256)S(1)}, s32[256]{0:T(256)}, u32[]{:S(2)}) copy-start(s32[256]{0:T(256)} %param.17) | copy-start | bytes 3076
  11.0 7.5 %copy-start.13 = (bf16[1536,4096]{1,0:T(8,128)(2,1)S(1)}, bf16[1536,4096]{1,0:T(8,128)(2,1)}, u32[]{:S(2)}) copy-start(bf16[1536,4096]{1,0:T(8,128)(2,1)} %param.20) | copy-start | bytes 37748740
  18.1 4.5 %slice-start = ((s8[6291456]{0:T(1024)(128)(4,1)}), s8[2097152]{0:T(1024)(128)(4,1)S(1)}, s32[]{:S(2)}) async-start(s8[6291456]{0:T(1024)(128)(4,1)} %bitcast.98), calls=%async_computation | async-start | bytes 4194304
  18.5 4.1 %slice-start.1 = ((s8[6291456]{0:T(1024)(128)(4,1)}), s8[4194304]{0:T(1024)(128)(4,1)S(1)}, s32[]{:S(2)}) async-start(s8[6291456]{0:T(1024)(128)(4,1)} %bitcast.98), calls=%async_computation.1 | async-start | bytes 8388608
  22.7 1.9 copy-start.12
  22.7 2.2 copy-start.5
  27.5 2.2 copy-start.6
  38.5 7.2 %collective-permute-start = (bf16[256,512]{1,0:T(8,128)(2,1)S(1)}, bf16[256,512]{1,0:T(8,128)(2,1)S(1)}, u32[]{:S(2)}, u32[]{:S(2)}) collective-permute-start(bf16[256,512]{1,0:T(8,128)(2,1)S(1)} %get-tuple-element.514), channel_id=1, source_target_pairs={{0,1},{1,2},{2,3},{3,0},{4,5},{5,6},{6,7},{7,4}} | collective-permute-start | bytes 786440 | tf_op jit(solution)/shard_map/while/body/eval_jaxpr/ppermute | solution.py:113
  39.3 6.3 %collective-permute-start.1 = (bf16[256,64]{0,1:T(8,128)(2,1)S(1)}, bf16[256,64]{0,1:T(8,128)(2,1)S(1)}, u32[]{:S(2)}, u32[]{:S(2)}) collective-permute-start(bf16[256,64]{0,1:T(8,128)(2,1)S(1)} %get-tuple-element.515), channel_id=1, source_target_pairs={{0,1},{1,2},{2,3},{3,0},{4,5},{5,6},{6,7},{7,4}} | collective-permute-start | bytes 98312 | tf_op jit(solution)/shard_map/while/body/eval_jaxpr/ppermute | solution.py:114
  51.9 2.2 copy-start.7
  54.1 2.2 copy-start.2
  61.7 6.2 %collective-permute-start = (bf16[256,512]{1,0:T(8,128)(2,1)S(1)}, bf16[256,512]{1,0:T(8,128)(2,1)S(1)}, u32[]{:S(2)}, u32[]{:S(2)}) collective-permute-start(bf16[256,512]{1,0:T(8,128)(2,1)S(1)} %get-tuple-element.514), channel_id=1, source_target_pairs={{0,1},{1,2},{2,3},{3,0},{4,5},{5,6},{6,7},{7,4}} | collective-permute-start | bytes 786440 | tf_op jit(solution)/shard_map/while/body/eval_jaxpr/ppermute | solution.py:113
  61.9 6.0 %collective-permute-start.1 = (bf16[256,64]{0,1:T(8,128)(2,1)S(1)}, bf16[256,64]{0,1:T(8,128)(2,1)S(1)}, u32[]{:S(2)}, u32[]{:S(2)}) collective-permute-start(bf16[256,64]{0,1:T(8,128)(2,1)S(1)} %get-tuple-element.515), channel_id=1, source_target_pairs={{0,1},{1,2},{2,3},{3,0},{4,5},{5,6},{6,7},{7,4}} | collective-permute-start | bytes 98312 | tf_op jit(solution)/shard_map/while/body/eval_jaxpr/ppermute | solution.py:114
  74.1 2.2 copy-start.7
  76.3 2.2 copy-start.2
  83.9 6.2 %collective-permute-start = (bf16[256,512]{1,0:T(8,128)(2,1)S(1)}, bf16[256,512]{1,0:T(8,128)(2,1)S(1)}, u32[]{:S(2)}, u32[]{:S(2)}) collective-permute-start(bf16[256,512]{1,0:T(8,128)(2,1)S(1)} %get-tuple-element.514), channel_id=1, source_target_pairs={{0,1},{1,2},{2,3},{3,0},{4,5},{5,6},{6,7},{7,4}} | collective-permute-start | bytes 786440 | tf_op jit(solution)/shard_map/while/body/eval_jaxpr/ppermute | solution.py:113
  84.1 6.0 %collective-permute-start.1 = (bf16[256,64]{0,1:T(8,128)(2,1)S(1)}, bf16[256,64]{0,1:T(8,128)(2,1)S(1)}, u32[]{:S(2)}, u32[]{:S(2)}) collective-permute-start(bf16[256,64]{0,1:T(8,128)(2,1)S(1)} %get-tuple-element.515), channel_id=1, source_target_pairs={{0,1},{1,2},{2,3},{3,0},{4,5},{5,6},{6,7},{7,4}} | collective-permute-start | bytes 98312 | tf_op jit(solution)/shard_map/while/body/eval_jaxpr/ppermute | solution.py:114
  96.3 2.2 copy-start.7
  98.5 2.2 copy-start.2
  106.1 171.8 %copy-start.1 = (bf16[256,6144]{1,0:T(8,128)(2,1)S(1)}, bf16[256,6144]{1,0:T(8,128)(2,1)}, u32[]{:S(2)}) copy-start(bf16[256,6144]{1,0:T(8,128)(2,1)} %param.16) | copy-start | bytes 9437188
where the time goes:
time: 279 us; the launch traced here: 278 us
  blocking collectives  148 us (53%)
  matrix products  85.8 us (31%)
  other arithmetic  12.1 us (4%)
  local copies, waits for them, and re-layouts  11.8 us (4%)
  waiting for transfers between devices  10.5 us (4%)
  starting transfers between devices  8.99 us (3%)
    psum x1, blocking collectives, local_step(): return lax.psum(y_part, 'tp').astype(jnp.bfloat16)  148 us
    dot_general x1, matrix products, local_step(): jnp.einsum('htv,hvd->td', attn_out, w_o.reshape(heads_loc, value_dim, -1)...  23.7 us
    dot_general x4, matrix products, block_stats(): jnp.einsum('hqk,khv->hqv', prob_tile.astype(jnp.bfloat16), v_rows, prefer...  12 us
    dot_general x4, matrix products, up_project(): jnp.dot(lat_rows, w_uk, preferred_element_type=jnp.float32)  11.7 us
    ppermute x3, waiting for transfers between devices, ctx_step(): rot_blk = lax.ppermute(rot_blk, 'ctx', next_perm)  10.5 us
    dot_general x1, matrix products, project_tokens(): jnp.dot(tok_x, w_dq, preferred_element_type=jnp.float32)  9.06 us
    ppermute x3, starting transfers between devices, ctx_step(): rot_blk = lax.ppermute(rot_blk, 'ctx', next_perm)  7.82 us
    dot_general x4, matrix products, block_scores(): jnp.einsum('qhn,khn->hqk', q_nope, k_nope, preferred_element_type=jnp.flo...  7.36 us
  transfers between devices with their start and end apart: 6, of which 3 were waited for; matrix products, arithmetic and copies ran while one was open for 0% of the time, Pallas kernels for 0%

commit v1 on v0

v1 whole, which is shorter than its diff:
```python
import functools

import jax
import jax.numpy as jnp
from jax import lax
from jax.experimental import pallas as pl
from jax.experimental.pallas import tpu as pltpu
from jax.sharding import PartitionSpec as P

ROPE_BASE = 10000.0
NORM_EPS = 1e-6
NEG_BIG = -1e30
MESH = pl.DeviceIdType.MESH
F32 = jnp.float32
BF16 = jnp.bfloat16

KCH = 6
NBLK = 256
RING = 3
WO_SLOTS = 9


def _dot(a, b):
    return jnp.dot(a, b, preferred_element_type=F32)


def _dot_nt(a, b):
    return lax.dot_general(a, b, (((1,), (1,)), ((), ())), preferred_element_type=F32)


def layer_kernel(dims, x_hbm, pos_ref, wdq_hbm, gq_ref, wuq_hbm, wqr_hbm, wdkv_hbm, gkv_ref, wkr_hbm, wuk_hbm, wuv_hbm,
                 wo_hbm, y_hbm,
                 xv, wkv, wkr, arena, lat, kplo, kphi, cq, accq, acckv, acckr, cosr, sinr,
                 uqb, qrb, ukb, uvb, ov, sendb, recvb, ownb, resb,
                 xsem, kvsem, krsem, bsem, csem, wosem, lats, latr, ps, pr, rs, rr, ys):
    D, QR, LR, HL, half, score_scale = dims
    nheads2 = HL // 2
    kc = D // KCH
    nb_q = QR // NBLK
    own_cols = D // 2
    nblk = own_cols // NBLK
    hv = HL * 128
    tp = lax.axis_index("tp")
    ci = lax.axis_index("ctx")
    xpeer = lax.rem(ci + 2, 4)
    dpeer = ci + 1 - 2 * lax.rem(ci, 2)

    def a_copies(k):
        col = pl.multiple_of(k * kc, 128)
        return (pltpu.make_async_copy(x_hbm.at[:, pl.ds(col, kc)], xv.at[:, pl.ds(col, kc)], xsem.at[k]),
                pltpu.make_async_copy(wdkv_hbm.at[pl.ds(col, kc), :], wkv.at[k], kvsem.at[k]),
                pltpu.make_async_copy(wkr_hbm.at[:, pl.ds(col, kc)], wkr.at[k], krsem.at[k]))

    def b_copy(n):
        return pltpu.make_async_copy(wdq_hbm.at[:, pl.ds(pl.multiple_of(n * NBLK, NBLK), NBLK)],
                                     arena.at[pl.ds(pl.multiple_of(n * D, D), D), :], bsem.at[n])

    def c_copies(g):
        hp = lax.rem(g, nheads2)
        s = lax.rem(g, RING)
        c2 = pl.ds(pl.multiple_of(hp * 256, 256), 256)
        c1 = pl.ds(pl.multiple_of(hp * 128, 128), 128)
        return (pltpu.make_async_copy(wuq_hbm.at[:, c2], uqb.at[s], csem.at[s, 0]),
                pltpu.make_async_copy(wqr_hbm.at[:, c1], qrb.at[s], csem.at[s, 1]),
                pltpu.make_async_copy(wuk_hbm.at[:, c2], ukb.at[s], csem.at[s, 2]),
                pltpu.make_async_copy(wuv_hbm.at[:, c2], uvb.at[s], csem.at[s, 3]))

    def wo_copy(L):
        j = lax.rem(L, nblk)
        side = jnp.where(L < 2 * nblk, 1 - tp, tp)
        s = lax.rem(L, WO_SLOTS)
        col = pl.multiple_of(side * own_cols + j * NBLK, NBLK)
        return pltpu.make_async_copy(wo_hbm.at[:, pl.ds(col, NBLK)],
                                     arena.at[pl.ds(pl.multiple_of(s * hv, hv), hv), :], wosem.at[s])

    def start(cps):
        for c in cps:
            c.start()

    def wait(cps):
        for c in cps:
            c.wait()

    for k in range(KCH):
        start(a_copies(k))
    b_copy(0).start()

    bar = pltpu.get_barrier_semaphore()
    for dev in ({"tp": 1 - tp}, {"ctx": xpeer}, {"ctx": dpeer}):
        pl.semaphore_signal(bar, inc=1, device_id=dev, device_id_type=MESH)

    lane = lax.broadcasted_iota(jnp.int32, (1, 128), 1)
    fidx = lax.rem(lane, 32)
    freq = jnp.zeros((1, 128), F32)
    for j in range(32):
        freq = jnp.where(fidx == j, ROPE_BASE ** (-j * 2.0 / 64), freq)
    first_half = lax.rem(lane, 64) < 32
    eye = lax.broadcasted_iota(jnp.int32, (128, 128), 0) == lax.broadcasted_iota(jnp.int32, (128, 128), 1)
    for hf in range(2):
        prow = pos_ref[hf:hf + 1, :].astype(F32)
        pcol = jnp.sum(jnp.where(eye, jnp.broadcast_to(prow, (128, 128)), 0.0), axis=1, keepdims=True)
        ang = pcol * freq
        cosr[hf * half:(hf + 1) * half, :] = jnp.cos(ang)
        sn = jnp.sin(ang)
        sinr[hf * half:(hf + 1) * half, :] = jnp.where(first_half, -sn, sn)

    def rope(a, row0):
        n = a.shape[0]
        swapped = jnp.where(first_half, pltpu.roll(a, 96, 1), pltpu.roll(a, 32, 1))
        return a * cosr[row0:row0 + n, :] + swapped * sinr[row0:row0 + n, :]

    acckv[...] = jnp.zeros_like(acckv)
    acckr[...] = jnp.zeros_like(acckr)

    def a_step(k, carry):
        @pl.when(k >= 1)
        def _():
            b_copy(k).start()
        wait(a_copies(k))
        xk = xv[:, pl.ds(pl.multiple_of(k * kc, 128), kc)]
        acckv[...] += _dot(xk, wkv[k])
        acckr[...] += _dot_nt(xk, wkr[k])
        return carry

    lax.fori_loop(0, KCH, a_step, 0)

    pieces = (ci, 7 - ci)

    def lat_rows(piece):
        return lat.at[pl.ds(pl.multiple_of(piece * half, half), half), :]

    def lat_send(piece, slot, dev):
        ref = lat_rows(piece)
        return pltpu.make_async_remote_copy(src_ref=ref, dst_ref=ref, send_sem=lats.at[slot], recv_sem=latr.at[piece],
                                            device_id={"ctx": dev}, device_id_type=MESH)

    gkv = gkv_ref[...].astype(F32)
    for hf in range(2):
        rows = slice(hf * half, (hf + 1) * half)
        a = acckv[rows, :]
        inv = lax.rsqrt(jnp.mean(a * a, axis=-1, keepdims=True) + NORM_EPS)
        kr = acckr[rows, :]
        kr2 = rope(jnp.concatenate([kr, kr], axis=1), hf * half)
        row0 = pl.multiple_of(pieces[hf] * half, half)
        lat[pl.ds(row0, half), 0:LR] = (a * inv * gkv).astype(BF16)
        lat[pl.ds(row0, half), LR:LR + 128] = kr2.astype(BF16)
        if hf == 0:
            pl.semaphore_wait(bar, 3)
        lat_send(pieces[hf], 2 * hf, xpeer).start()
        lat_send(pieces[hf], 2 * hf + 1, dpeer).start()

    def b_step(n, carry):
        @pl.when(n >= nb_q - RING)
        def _():
            start(c_copies(n - (nb_q - RING)))
        b_copy(n).wait()
        w = arena[pl.ds(pl.multiple_of(n * D, D), D), :]
        accq[:, pl.ds(pl.multiple_of(n * NBLK, NBLK), NBLK)] = _dot(xv[...], w)
        return carry

    lax.fori_loop(0, nb_q, b_step, 0)
    gq = gq_ref[...].astype(F32)
    aq = accq[...]
    invq = lax.rsqrt(jnp.mean(aq * aq, axis=-1, keepdims=True) + NORM_EPS)
    cq[...] = (aq * invq * gq).astype(BF16)

    far = (xpeer, 7 - xpeer)
    near = (dpeer, 7 - dpeer)
    relayed = (3 - ci, 4 + ci)

    def lat_recv(piece):
        lat_send(piece, 0, dpeer).wait_recv()

    def relay(hf):
        lat_recv(far[hf])
        lat_send(far[hf], 4 + hf, dpeer).start()
        lat_recv(near[hf])
        lat_recv(relayed[hf])
        rows = slice(hf * 4 * half, (hf + 1) * 4 * half)
        kp = lat[rows, LR:LR + 128].astype(F32)
        low = lane < 64
        kplo[rows, :] = jnp.where(low, kp, 0.0).astype(BF16)
        kphi[rows, :] = jnp.where(low, 0.0, kp).astype(BF16)

    def heads(chunk, nk, q_index):
        rows = slice(chunk * half, (chunk + 1) * half)
        base = q_index * half

        def body(hp, carry):
            g = hp + chunk * nheads2
            s = lax.rem(g, RING)
            wait(c_copies(g))
            c = cq[rows, :]
            qn = _dot(c, uqb[s]).astype(BF16)
            qp = rope(_dot(c, qrb[s]), chunk * half).astype(BF16)
            lt = lat[0:nk, 0:LR]
            kn = _dot(lt, ukb[s]).astype(BF16)
            vv = _dot(lt, uvb[s]).astype(BF16)

            @pl.when(g + RING < 2 * nheads2)
            def _():
                start(c_copies(g + RING))
            if chunk == 0:
                @pl.when(lax.rem(hp, 2) == 0)
                def _():
                    wo_copy(lax.div(hp, 2)).start()
            vis = (lax.broadcasted_iota(jnp.int32, (half, nk), 1)
                   <= lax.broadcasted_iota(jnp.int32, (half, nk), 0) + base)
            for h in range(2):
                kp = kplo if h == 0 else kphi
                qh = jnp.concatenate([qn[:, h * 128:(h + 1) * 128], qp], axis=1)
                kh = jnp.concatenate([kn[:, h * 128:(h + 1) * 128], kp[0:nk, :]], axis=1)
                sc = jnp.where(vis, _dot_nt(qh, kh), NEG_BIG)
                top = jnp.max(sc, axis=1, keepdims=True)
                p = jnp.exp((sc - top) * score_scale)
                tot = jnp.sum(p, axis=1, keepdims=True)
                acc = _dot(p.astype(BF16), vv[:, h * 128:(h + 1) * 128])
                ov[rows, pl.ds(pl.multiple_of(hp * 256 + h * 128, 128), 128)] = (acc / tot).astype(BF16)
            return carry

        lax.fori_loop(0, nheads2, body, 0)

    def part_send(t):
        return pltpu.make_async_remote_copy(src_ref=sendb.at[t], dst_ref=recvb.at[t], send_sem=ps.at[t], recv_sem=pr.at[t],
                                            device_id={"tp": 1 - tp}, device_id_type=MESH)

    total_wo = 3 * nblk
    ahead = WO_SLOTS - 1

    def wo_block(L):
        wo_copy(L).wait()
        s = lax.rem(L, WO_SLOTS)
        return arena[pl.ds(pl.multiple_of(s * hv, hv), hv), :]

    def wo_next(L):
        @pl.when(L + ahead < total_wo)
        def _():
            wo_copy(L + ahead).start()

    def project_partner(chunk):
        rows = slice(chunk * half, (chunk + 1) * half)

        def body(j, carry):
            t = chunk * nblk + j
            wo_next(t)
            sendb[t] = _dot(ov[rows, :], wo_block(t))
            part_send(t).start()
            return carry

        lax.fori_loop(0, nblk, body, 0)

    relay(0)
    heads(0, 4 * half, ci)
    project_partner(0)
    relay(1)
    heads(1, 8 * half, 7 - ci)
    project_partner(1)

    def own_body(j, carry):
        L = 2 * nblk + j
        wo_next(L)
        r = _dot(ov[...], wo_block(L))
        ownb[j] = r[:half]
        ownb[nblk + j] = r[half:]
        return carry

    lax.fori_loop(0, nblk, own_body, 0)

    def y_block(t, side):
        c = lax.div(t, nblk)
        j = lax.rem(t, nblk)
        return y_hbm.at[pl.ds(pl.multiple_of(c * half, half), half),
                        pl.ds(pl.multiple_of(side * own_cols + j * NBLK, NBLK), NBLK)]

    def result_send(t):
        return pltpu.make_async_remote_copy(src_ref=resb.at[t], dst_ref=y_block(t, tp), send_sem=rs.at[t], recv_sem=rr.at[t],
                                            device_id={"tp": 1 - tp}, device_id_type=MESH)

    def result_store(t):
        return pltpu.make_async_copy(resb.at[t], y_block(t, tp), ys.at[t])

    def ret_body(t, carry):
        part_send(t).wait_recv()
        resb[t] = (recvb[t] + ownb[t]).astype(BF16)
        result_send(t).start()
        result_store(t).start()
        return carry

    lax.fori_loop(0, 2 * nblk, ret_body, 0)

    def drain(t, carry):
        part_send(t).wait_send()
        result_send(t).wait_send()
        result_store(t).wait()
        pltpu.make_async_remote_copy(src_ref=resb.at[t], dst_ref=y_block(t, 1 - tp), send_sem=rs.at[t], recv_sem=rr.at[t],
                                     device_id={"tp": 1 - tp}, device_id_type=MESH).wait_recv()
        return carry

    lax.fori_loop(0, 2 * nblk, drain, 0)
    for slot, piece in ((0, pieces[0]), (1, pieces[0]), (2, pieces[1]), (3, pieces[1]), (4, far[0]), (5, far[1])):
        lat_send(piece, slot, dpeer).wait_send()


def solution(mesh):
    tok_spec = P(('dp', 'ctx'), None)
    pos_spec = P(('dp', 'ctx'))
    full_mat = P(None, None)
    full_vec = P(None)
    col_spec = P(None, 'tp')
    row_spec = P('tp', None)

    def local_step(tok_x, tok_pos, w_dq, g_q, w_uq, w_qr, w_dkv, g_kv, w_kr, w_uk, w_uv, w_o):
        rows, D = tok_x.shape
        half = rows // 2
        QR = w_dq.shape[1]
        LR = w_dkv.shape[1]
        HL = w_qr.shape[1] // w_kr.shape[1]
        scale = (128 + w_kr.shape[1]) ** -0.5
        nblk = D // 2 // NBLK
        kc = D // KCH
        ntok = 8 * half
        dims = (D, QR, LR, HL, half, scale)
        anyspec = pl.BlockSpec(memory_space=pl.ANY)
        vspec = pl.BlockSpec(memory_space=pltpu.VMEM)
        dma = pltpu.SemaphoreType.DMA
        arena_rows = max(QR // NBLK * D, WO_SLOTS * HL * 128)
        return pl.pallas_call(
            functools.partial(layer_kernel, dims),
            out_shape=jax.ShapeDtypeStruct((rows, D), BF16),
            in_specs=[anyspec, vspec, anyspec, vspec, anyspec, anyspec, anyspec, vspec, anyspec, anyspec, anyspec, anyspec],
            out_specs=anyspec,
            scratch_shapes=[
                pltpu.VMEM((rows, D), BF16),
                pltpu.VMEM((KCH, kc, LR), BF16),
                pltpu.VMEM((KCH, 64, kc), BF16),
                pltpu.VMEM((arena_rows, NBLK), BF16),
                pltpu.VMEM((ntok, LR + 128), BF16),
                pltpu.VMEM((ntok, 128), BF16),
                pltpu.VMEM((ntok, 128), BF16),
                pltpu.VMEM((rows, QR), BF16),
                pltpu.VMEM((rows, QR), F32),
                pltpu.VMEM((rows, LR), F32),
                pltpu.VMEM((rows, 64), F32),
                pltpu.VMEM((rows, 128), F32),
                pltpu.VMEM((rows, 128), F32),
                pltpu.VMEM((RING, QR, 256), BF16),
                pltpu.VMEM((RING, QR, 128), BF16),
                pltpu.VMEM((RING, LR, 256), BF16),
                pltpu.VMEM((RING, LR, 256), BF16),
                pltpu.VMEM((rows, HL * 128), BF16),
                pltpu.VMEM((2 * nblk, half, NBLK), F32),
                pltpu.VMEM((2 * nblk, half, NBLK), F32),
                pltpu.VMEM((2 * nblk, half, NBLK), F32),
                pltpu.VMEM((2 * nblk, half, NBLK), BF16),
                dma((KCH,)), dma((KCH,)), dma((KCH,)), dma((QR // NBLK,)), dma((RING, 4)), dma((WO_SLOTS,)),
                dma((6,)), dma((8,)), dma((2 * nblk,)), dma((2 * nblk,)), dma((2 * nblk,)), dma((2 * nblk,)), dma((2 * nblk,)),
            ],
            compiler_params=pltpu.CompilerParams(collective_id=0, has_side_effects=True,
                                                 vmem_limit_bytes=60 * 1024 * 1024),
        )(tok_x, tok_pos.reshape(2, half), w_dq, g_q.reshape(1, QR), w_uq, w_qr, w_dkv, g_kv.reshape(1, LR), w_kr.T,
          w_uk, w_uv, w_o)

    return jax.shard_map(local_step, mesh=mesh,
                         in_specs=(tok_spec, pos_spec, full_mat, full_vec, col_spec, col_spec, full_mat, full_vec, full_mat, col_spec, col_spec, row_spec),
                         out_specs=tok_spec, check_vma=False)
```

time: 279 us -> 152 us (0.54)
  blocking collectives: 148 us -> 0 us
  Pallas kernels: 0 us -> 145 us
  matrix products: 85.8 us -> 0 us
  other arithmetic: 12.1 us -> 0 us
  waiting for transfers between devices: 10.5 us -> 0 us
  starting transfers between devices: 8.99 us -> 0 us
  local copies, waits for them, and re-layouts: 11.8 us -> 6.42 us
    psum x1 -> x0, blocking collectives: 148 us -> none  [local_step(): return lax.psum(y_part, 'tp').astype(jnp.bfloat16)]
    pallas_call x0 -> x1, Pallas kernels: none -> 145 us  [local_step(): pl.pallas_call(functools.partial(layer_kernel, dims), out_shape=jax.Shape...]
    dot_general x26 -> x0, matrix products: 85.8 us -> none  [the longest x1 23.7 us: local_step(): jnp.einsum('htv,hvd->td', attn_out, w_o.reshape(heads_loc, value_dim, -1)...]
    ppermute x6 -> x0, waiting for transfers between devices: 10.5 us -> none  [the longest x3 10.5 us: ctx_step(): rot_blk = lax.ppermute(rot_blk, 'ctx', next_perm)]
    ppermute x6 -> x0, starting transfers between devices: 8.99 us -> none  [the longest x3 7.82 us: ctx_step(): rot_blk = lax.ppermute(rot_blk, 'ctx', next_perm)]
    concatenate x8 -> x0, other arithmetic: 7.31 us -> none  [the longest x3 7.21 us: attend_upper(): jnp.concatenate([old_acc[:, :half_len], top_acc], axis=1)]
    cond x12 -> x0, local copies, waits for them, and re-layouts: 6.84 us -> none
    reduce_sum x4 -> x0, other arithmetic: 3.92 us -> none  [block_stats(): blk_sum = jnp.sum(prob_tile, axis=-1)]
  transfers between devices with their start and end apart: 6 -> 0, of which waited for: 3 -> 0; matrix products, arithmetic and copies ran while one was open for 0% -> 0% of each run, Pallas kernels for 0% -> 0%
where the time goes in v1:
time: 152 us; the launch traced here: 151 us
  Pallas kernels  145 us (95%)
  local copies, waits for them, and re-layouts  6.42 us (4%)
    pallas_call x1, Pallas kernels, local_step(): pl.pallas_call(functools.partial(layer_kernel, dims), out_shape=jax.Shape...  145 us
    unnamed x1, local copies, waits for them, and re-layouts  3.88 us

profile of v1, /device:TPU:0, one launch (start us, length us, event | category | flops | bytes accessed | tf_op | source)
XLA Modules:
  0.0 151.3 jit_solution(11329618976088938609)
XLA Ops:
  0.0 1.3 reshape.11.gkv_ref
  1.3 1.3 reshape.10.gq_ref
  2.5 144.9 %shard_map.118 = bf16[256,6144]{1,0:T(8,128)(2,1)} custom-call(bf16[256,6144]{1,0:T(8,128)(2,1)} %x_hbm.1, s32[2,128]{1,0:T(2,128)} %bitcast.3, bf16[6144,1536]{1,0:T(8,128)(2,1)} %wdq_hbm.1, bf16[1,1536]{1,0:T(2,128)(2,1)} %reshape.10.gq_ref, bf16[1536,4096]{1,0:T(8,128)(2,1)} %wuq_hbm.1, bf16[1536,2048]{1,0:T(8,128)(2,1)} %wqr_hbm.1, ...), custom_call_target="tpu_custom_call" | custom-call | tf_op jit(solution)/shard_map/pallas_call | solution.py:327
  147.5 3.9 %copy.14 = bf16[256,6144]{1,0:T(8,128)(2,1)} copy(bf16[256,6144]{1,0:T(8,128)(2,1)} %shard_map.118) | data formatting | bytes 6291456

commit v2 on v1

v2 whole, which is shorter than its diff:
```python
import functools

import jax
import jax.numpy as jnp
from jax import lax
from jax.experimental import pallas as pl
from jax.experimental.pallas import tpu as pltpu
from jax.sharding import PartitionSpec as P

ROPE_BASE = 10000.0
NORM_EPS = 1e-6
NEG_BIG = -1e30
MESH = pl.DeviceIdType.MESH
F32 = jnp.float32
BF16 = jnp.bfloat16

KCH = 6
NBLK = 256
RING = 3
WO_SLOTS = 9


def _dot(a, b):
    return jnp.dot(a, b, preferred_element_type=F32)


def _dot_nt(a, b):
    return lax.dot_general(a, b, (((1,), (1,)), ((), ())), preferred_element_type=F32)


def layer_kernel(dims, x_hbm, pos_ref, wdq_hbm, gq_ref, wuq_hbm, wqr_hbm, wdkv_hbm, gkv_ref, wkr_hbm, wuk_hbm, wuv_hbm,
                 wo_hbm, y_hbm,
                 xv, kvs, wkr, upw, arena, lat, kplo, kphi, cq, acckv, acckr, rot,
                 uqb, qrb, qn, qp, os, orx, sendb, recvb, ownb, resb,
                 xsem, kvsem, krsem, bsem, qsem, upsem, wosem, lats, latr, cqs, cqr, rots, rotr, oss, osr, ps, pr, rs, rr, ys):
    D, QR, LR, HL, half, score_scale = dims
    HC = HL // 2
    ngrp = HC // 4
    kc = D // KCH
    nb_q = QR // NBLK
    own_cols = D // 2
    nblk = own_cols // NBLK
    hv = HL * 128
    ntok = 8 * half
    tp = lax.axis_index("tp")
    ci = lax.axis_index("ctx")
    core = lax.rem(ci, 2)
    xpeer = lax.rem(ci + 2, 4)
    dpeer = ci + 1 - 2 * core
    pieces = (ci, 7 - ci)
    mine = tuple(pl.ds(pl.multiple_of(sl * half, half), half) for sl in (core, 1 - core))
    theirs = tuple(pl.ds(pl.multiple_of(sl * half, half), half) for sl in (1 - core, core))
    first_pos = (2 * half * lax.div(ci, 2), half * (6 - 2 * lax.div(ci, 2)))
    half_rows = (slice(0, half), slice(half, 2 * half))

    def x_copy(hf, k):
        col = pl.multiple_of(k * kc, 128)
        rows = pl.ds(hf * half, half)
        return pltpu.make_async_copy(x_hbm.at[rows, pl.ds(col, kc)], xv.at[rows, pl.ds(col, kc)], xsem.at[hf, k])

    def a_copies(k):
        col = pl.multiple_of(k * kc, 128)
        return (pltpu.make_async_copy(wkr_hbm.at[:, pl.ds(col, kc)], wkr.at[:, pl.ds(col, kc)], krsem.at[k]),
                pltpu.make_async_copy(wdkv_hbm.at[pl.ds(col, kc), :], kvs.at[pl.ds(col, kc), :], kvsem.at[k]))

    def b_copy(n):
        return pltpu.make_async_copy(wdq_hbm.at[:, pl.ds(pl.multiple_of(n * NBLK, NBLK), NBLK)],
                                     arena.at[pl.ds(pl.multiple_of(n * D, D), D), :], bsem.at[n])

    def q_copies(g):
        i = lax.rem(g, ngrp) + core * ngrp
        s = lax.rem(g, RING)
        c4 = pl.ds(pl.multiple_of(i * 512, 512), 512)
        c2 = pl.ds(pl.multiple_of(i * 256, 256), 256)
        return (pltpu.make_async_copy(wuq_hbm.at[:, c4], uqb.at[s], qsem.at[s, 0]),
                pltpu.make_async_copy(wqr_hbm.at[:, c2], qrb.at[s], qsem.at[s, 1]))

    def up_copies(i):
        c4 = pl.ds(pl.multiple_of((i + core * ngrp) * 512, 512), 512)
        return (pltpu.make_async_copy(wuk_hbm.at[:, c4], upw.at[i], upsem.at[i, 0]),
                pltpu.make_async_copy(wuv_hbm.at[:, c4], upw.at[ngrp + i], upsem.at[i, 1]))

    def wo_copy(L):
        j = lax.rem(L, nblk)
        side = jnp.where(L < 2 * nblk, 1 - tp, tp)
        s = lax.rem(L, WO_SLOTS)
        col = pl.multiple_of(side * own_cols + j * NBLK, NBLK)
        return pltpu.make_async_copy(wo_hbm.at[:, pl.ds(col, NBLK)],
                                     arena.at[pl.ds(pl.multiple_of(s * hv, hv), hv), :], wosem.at[s])

    def start(cps):
        for c in cps:
            c.start()

    def wait(cps):
        for c in cps:
            c.wait()

    for k in range(KCH):
        x_copy(0, k).start()
        start(a_copies(k))
    for k in range(KCH):
        x_copy(1, k).start()

    bar = pltpu.get_barrier_semaphore()
    for dev in ({"tp": 1 - tp}, {"ctx": xpeer}, {"ctx": dpeer}):
        pl.semaphore_signal(bar, inc=1, device_id=dev, device_id_type=MESH)

    lane = lax.broadcasted_iota(jnp.int32, (1, 128), 1)
    first_half = lax.rem(lane, 64) < 32

    def rotary(hf):
        fidx = lax.rem(lane, 32)
        freq = jnp.zeros((1, 128), F32)
        for j in range(32):
            freq = jnp.where(fidx == j, ROPE_BASE ** (-j * 2.0 / 64), freq)
        eye = (lax.broadcasted_iota(jnp.int32, (half, half), 0) == lax.broadcasted_iota(jnp.int32, (half, half), 1))
        prow = pos_ref[hf:hf + 1, :].astype(F32)
        pcol = jnp.sum(jnp.where(eye, jnp.broadcast_to(prow, (half, half)), 0.0), axis=1, keepdims=True)
        ang = pcol * freq
        rot[hf, mine[hf], 0:128] = jnp.cos(ang)
        sn = jnp.sin(ang)
        rot[hf, mine[hf], 128:256] = jnp.where(first_half, -sn, sn)

    def turn(a, table):
        swapped = jnp.where(first_half, pltpu.roll(a, 96, 1), pltpu.roll(a, 32, 1))
        return a * table[:, 0:128] + swapped * table[:, 128:256]

    def to_core(ref, ssem, rsem):
        return pltpu.make_async_remote_copy(src_ref=ref, dst_ref=ref, send_sem=ssem, recv_sem=rsem,
                                            device_id={"ctx": dpeer}, device_id_type=MESH)

    def rot_send(hf):
        return to_core(rot.at[hf, mine[hf], :], rots.at[hf], rotr.at[hf])

    def rot_recv(hf):
        return to_core(rot.at[hf, theirs[hf], :], rots.at[hf], rotr.at[hf])

    def lat_send(piece, slot, dev):
        ref = lat.at[pl.ds(pl.multiple_of(piece * half, half), half), :]
        return pltpu.make_async_remote_copy(src_ref=ref, dst_ref=ref, send_sem=lats.at[slot], recv_sem=latr.at[piece],
                                            device_id={"ctx": dev}, device_id_type=MESH)

    def lat_finish(hf, a, kr):
        inv = lax.rsqrt(jnp.mean(a * a, axis=-1, keepdims=True) + NORM_EPS)
        kr2 = turn(jnp.concatenate([kr, kr], axis=1), rot[hf, mine[hf], :])
        row0 = pl.multiple_of(pieces[hf] * half, half)
        for c in range(LR // 128):
            cols = slice(c * 128, (c + 1) * 128)
            lat[pl.ds(row0, half), cols] = (a[:, cols] * inv * gkv_ref[c:c + 1, :].astype(F32)).astype(BF16)
        lat[pl.ds(row0, half), LR:LR + 128] = kr2.astype(BF16)

    def lat_share(hf):
        lat_send(pieces[hf], 2 * hf, xpeer).start()
        lat_send(pieces[hf], 2 * hf + 1, dpeer).start()

    far = (xpeer, 7 - xpeer)
    near = (dpeer, 7 - dpeer)
    relayed = (3 - ci, 4 + ci)

    def lat_recv(piece):
        lat_send(piece, 0, dpeer).wait_recv()

    def forward(hf):
        lat_recv(far[hf])
        lat_send(far[hf], 4 + hf, dpeer).start()

    def gathered(hf):
        lat_recv(near[hf])
        lat_recv(relayed[hf])
        rows = slice(hf * 4 * half, (hf + 1) * 4 * half)
        kp = lat[rows, LR:LR + 128].astype(F32)
        low = lane < 64
        kplo[rows, :] = jnp.where(low, kp, 0.0).astype(BF16)
        kphi[rows, :] = jnp.where(low, 0.0, kp).astype(BF16)

    def qlat_finish(hf):
        sq = 0.0
        for n in range(nb_q):
            a = ownb[hf * nb_q + n]
            sq = sq + jnp.sum(a * a, axis=-1, keepdims=True)
        inv = lax.rsqrt(sq * (1.0 / QR) + NORM_EPS)
        for n in range(nb_q):
            a = ownb[hf * nb_q + n] * inv
            for u in range(NBLK // 128):
                c = n * (NBLK // 128) + u
                cq[hf, mine[hf], c * 128:(c + 1) * 128] = (
                    a[:, u * 128:(u + 1) * 128] * gq_ref[c:c + 1, :].astype(F32)).astype(BF16)

    def cq_send(hf):
        return to_core(cq.at[hf, mine[hf], :], cqs.at[hf], cqr.at[hf])

    def cq_recv(hf):
        return to_core(cq.at[hf, theirs[hf], :], cqs.at[hf], cqr.at[hf])

    def queries(chunk):
        def body(i, carry):
            g = i + chunk * ngrp
            s = lax.rem(g, RING)
            wait(q_copies(g))
            c = cq[chunk]
            r = _dot(c, qrb[s])
            qn[:, pl.ds(pl.multiple_of(i * 512, 512), 512)] = _dot(c, uqb[s]).astype(BF16)
            for u in range(2):
                qp[:, pl.ds(pl.multiple_of(i * 256 + u * 128, 128), 128)] = turn(r[:, u * 128:(u + 1) * 128], rot[chunk]).astype(BF16)

            @pl.when(g + RING < 2 * ngrp)
            def _():
                start(q_copies(g + RING))
            return carry

        lax.fori_loop(0, ngrp, body, 0)

    def kv_rows(i, n):
        return pl.ds(pl.multiple_of(i * ntok, ntok), n)

    def keys_values(chunk, nk):
        def body(i, carry):
            if chunk == 0:
                wait(up_copies(i))
            lt = lat[0:nk, 0:LR]
            kvs[kv_rows(i, nk), :] = _dot(lt, upw[i]).astype(BF16)
            kvs[kv_rows(ngrp + i, nk), :] = _dot(lt, upw[ngrp + i]).astype(BF16)
            return carry

        lax.fori_loop(0, ngrp, body, 0)

    c2e = score_scale * 1.4426950408889634

    def o_send(chunk, i):
        cols = pl.ds(pl.multiple_of(i * 512, 512), 512)
        return pltpu.make_async_remote_copy(src_ref=os.at[chunk, theirs[chunk], cols], dst_ref=orx.at[chunk, :, cols],
                                            send_sem=oss.at[chunk, i], recv_sem=osr.at[chunk, i],
                                            device_id={"ctx": dpeer}, device_id_type=MESH)

    def attention(chunk, nk):
        nq = 2 * half

        def body(i, carry):
            if chunk == 0:
                wo_copy(2 * i).start()
                wo_copy(2 * i + 1).start()
            vis = (lax.broadcasted_iota(jnp.int32, (nq, nk), 1)
                   <= lax.broadcasted_iota(jnp.int32, (nq, nk), 0) + first_pos[chunk])

            def scores(h):
                kp = kphi if h % 2 else kplo
                qpe = qp[:, pl.ds(pl.multiple_of(i * 256 + (h // 2) * 128, 128), 128)]
                qh = jnp.concatenate([qn[:, pl.ds(pl.multiple_of(i * 512 + h * 128, 128), 128)], qpe], axis=1)
                kh = jnp.concatenate([kvs[kv_rows(i, nk), h * 128:(h + 1) * 128], kp[0:nk, :]], axis=1)
                return _dot_nt(qh, kh)

            def values(h, sc):
                sc = jnp.where(vis, sc, NEG_BIG)
                top = jnp.max(sc, axis=1, keepdims=True)
                p = jnp.exp2((sc - top) * c2e)
                tot = jnp.sum(p, axis=1, keepdims=True)
                acc = _dot(p.astype(BF16), kvs[kv_rows(ngrp + i, nk), h * 128:(h + 1) * 128])
                os[chunk, :, pl.ds(pl.multiple_of(i * 512 + h * 128, 128), 128)] = (acc / tot).astype(BF16)

            sc = scores(0)
            for h in range(4):
                nxt = scores(h + 1) if h < 3 else None
                values(h, sc)
                sc = nxt
            o_send(chunk, i).start()
            return carry

        lax.fori_loop(0, ngrp, body, 0)

        def arrive(i, carry):
            o_send(chunk, i).wait_recv()
            return carry

        lax.fori_loop(0, ngrp, arrive, 0)

    total_wo = 3 * nblk
    ahead = WO_SLOTS - 1
    hc = HC * 128

    def wo_next(L):
        wo_copy(L).wait()

        @pl.when(L + ahead < total_wo)
        def _():
            wo_copy(L + ahead).start()

    def project(chunk, L):
        base = lax.rem(L, WO_SLOTS) * hv
        w_here = arena[pl.ds(pl.multiple_of(base + core * hc, hc), hc), :]
        w_there = arena[pl.ds(pl.multiple_of(base + (1 - core) * hc, hc), hc), :]
        return _dot(os[chunk, mine[chunk], :], w_here) + _dot(orx[chunk], w_there)

    def part_send(t):
        return pltpu.make_async_remote_copy(src_ref=sendb.at[lax.rem(t, nblk)], dst_ref=recvb.at[t], send_sem=ps.at[t],
                                            recv_sem=pr.at[t],
                                            device_id={"tp": 1 - tp}, device_id_type=MESH)

    def project_partner(chunk):
        def body(j, carry):
            t = chunk * nblk + j
            wo_next(t)
            if chunk == 1:
                part_send(j).wait_send()
            sendb[j] = project(chunk, t)
            part_send(t).start()
            return carry

        lax.fori_loop(0, nblk, body, 0)

    def y_block(chunk, j, side):
        return y_hbm.at[pl.ds(chunk * half, half), pl.ds(pl.multiple_of(side * own_cols + j * NBLK, NBLK), NBLK)]

    def result_send(chunk, j, side):
        t = chunk * nblk + j
        return pltpu.make_async_remote_copy(src_ref=resb.at[t], dst_ref=y_block(chunk, j, side), send_sem=rs.at[t],
                                            recv_sem=rr.at[t], device_id={"tp": 1 - tp}, device_id_type=MESH)

    def result_store(chunk, j):
        t = chunk * nblk + j
        return pltpu.make_async_copy(resb.at[t], y_block(chunk, j, tp), ys.at[t])

    def give_back(chunk, j, own):
        t = chunk * nblk + j
        part_send(t).wait_recv()
        resb[t] = (recvb[t] + own).astype(BF16)
        result_send(chunk, j, tp).start()
        result_store(chunk, j).start()

    acckv[...] = jnp.zeros_like(acckv)
    acckr[...] = jnp.zeros_like(acckr)
    with jax.named_scope('rot0'):
        rotary(0)

    def a_step(k, carry):
        x_copy(0, k).wait()
        wait(a_copies(k))

        @pl.when(k % 2 == 1)
        def _():
            b_copy(lax.div(k, 2)).start()
        cols = pl.ds(pl.multiple_of(k * kc, 128), kc)
        xk = xv[half_rows[0], cols]
        acckv[...] += _dot(xk, kvs[cols, :])
        acckr[...] += _dot_nt(xk, wkr[:, cols])
        return carry

    with jax.named_scope('lat0'):
        lax.fori_loop(0, KCH, a_step, 0)
        lat_finish(0, acckv[...], acckr[...])
        pl.semaphore_wait(bar, 3)
        lat_share(0)
        rot_send(0).start()
    with jax.named_scope('rot1'):
        rotary(1)
        rot_send(1).start()
        for k in range(KCH):
            x_copy(1, k).wait()

    def b_step(n, carry):
        b_copy(n).wait()

        @pl.when(n < nb_q - 3)
        def _():
            b_copy(n + 3).start()

        @pl.when(n < ngrp)
        def _():
            start(up_copies(n))

        @pl.when(n >= nb_q - RING)
        def _():
            start(q_copies(n - (nb_q - RING)))
        w = arena[pl.ds(pl.multiple_of(n * D, D), D), :]
        r = _dot(xv[...], w)
        ownb[n] = r[:half]
        ownb[nb_q + n] = r[half:]
        return carry

    with jax.named_scope('qlat'):
        lax.fori_loop(0, nb_q, b_step, 0)
    with jax.named_scope('qfin'):
        forward(0)
        qlat_finish(0)
        cq_send(0).start()
    with jax.named_scope('lat1'):
        xs = xv[half_rows[1], :]
        lat_finish(1, _dot(xs, kvs[0:D, :]), _dot_nt(xs, wkr[...]))
        lat_share(1)
        qlat_finish(1)
        cq_send(1).start()
    with jax.named_scope('gather0'):
        gathered(0)
    with jax.named_scope('kv0'):
        keys_values(0, 4 * half)
    with jax.named_scope('q0'):
        cq_recv(0).wait_recv()
        rot_recv(0).wait_recv()
        queries(0)
    with jax.named_scope('att0'):
        attention(0, 4 * half)
    with jax.named_scope('part0'):
        project_partner(0)
    with jax.named_scope('gather1'):
        forward(1)
        gathered(1)
    with jax.named_scope('kv1'):
        keys_values(1, 8 * half)
    with jax.named_scope('q1'):
        cq_recv(1).wait_recv()
        rot_recv(1).wait_recv()
        queries(1)
    with jax.named_scope('att1'):
        attention(1, 8 * half)
    with jax.named_scope('part1'):
        project_partner(1)

    def own_body(j, carry):
        L = 2 * nblk + j
        wo_next(L)
        ownb[j] = project(1, L)
        give_back(0, j, project(0, L))
        return carry

    with jax.named_scope('own'):
        lax.fori_loop(0, nblk, own_body, 0)

    def ret_body(j, carry):
        give_back(1, j, ownb[j])
        return carry

    with jax.named_scope('ret'):
        lax.fori_loop(0, nblk, ret_body, 0)

    def drain(j, carry):
        part_send(nblk + j).wait_send()
        for chunk in range(2):
            result_send(chunk, j, tp).wait_send()
            result_store(chunk, j).wait()
            result_send(chunk, j, 1 - tp).wait_recv()
        return carry

    with jax.named_scope('drain'):
        lax.fori_loop(0, nblk, drain, 0)
    for slot, piece in ((0, pieces[0]), (1, pieces[0]), (2, pieces[1]), (3, pieces[1]), (4, far[0]), (5, far[1])):
        lat_send(piece, slot, dpeer).wait_send()
    for hf in range(2):
        rot_send(hf).wait_send()
        cq_send(hf).wait_send()
        for i in range(ngrp):
            o_send(hf, i).wait_send()


def solution(mesh):
    tok_spec = P(('dp', 'ctx'), None)
    pos_spec = P(('dp', 'ctx'))
    full_mat = P(None, None)
    full_vec = P(None)
    col_spec = P(None, 'tp')
    row_spec = P('tp', None)

    def local_step(tok_x, tok_pos, w_dq, g_q, w_uq, w_qr, w_dkv, g_kv, w_kr, w_uk, w_uv, w_o):
        rows, D = tok_x.shape
        half = rows // 2
        QR = w_dq.shape[1]
        LR = w_dkv.shape[1]
        HL = w_qr.shape[1] // w_kr.shape[1]
        scale = (128 + w_kr.shape[1]) ** -0.5
        nblk = D // 2 // NBLK
        ngrp = HL // 8
        ntok = 8 * half
        dims = (D, QR, LR, HL, half, scale)
        anyspec = pl.BlockSpec(memory_space=pl.ANY)
        vspec = pl.BlockSpec(memory_space=pltpu.VMEM)
        dma = pltpu.SemaphoreType.DMA
        arena_rows = max(QR // NBLK * D, WO_SLOTS * HL * 128)
        return pl.pallas_call(
            functools.partial(layer_kernel, dims),
            out_shape=jax.ShapeDtypeStruct((rows, D), BF16),
            in_specs=[anyspec, vspec, anyspec, vspec, anyspec, anyspec, anyspec, vspec, anyspec, anyspec, anyspec, anyspec],
            out_specs=anyspec,
            scratch_shapes=[
                pltpu.VMEM((rows, D), BF16),
                pltpu.VMEM((max(D, 2 * ngrp * ntok), LR), BF16),
                pltpu.VMEM((64, D), BF16),
                pltpu.VMEM((2 * ngrp, LR, 512), BF16),
                pltpu.VMEM((arena_rows, NBLK), BF16),
                pltpu.VMEM((ntok, LR + 128), BF16),
                pltpu.VMEM((ntok, 128), BF16),
                pltpu.VMEM((ntok, 128), BF16),
                pltpu.VMEM((2, rows, QR), BF16),
                pltpu.VMEM((half, LR), F32),
                pltpu.VMEM((half, 64), F32),
                pltpu.VMEM((2, rows, 256), F32),
                pltpu.VMEM((RING, QR, 512), BF16),
                pltpu.VMEM((RING, QR, 256), BF16),
                pltpu.VMEM((rows, HL * 64), BF16),
                pltpu.VMEM((rows, HL * 32), BF16),
                pltpu.VMEM((2, rows, HL * 64), BF16),
                pltpu.VMEM((2, half, HL * 64), BF16),
                pltpu.VMEM((nblk, half, NBLK), F32),
                pltpu.VMEM((2 * nblk, half, NBLK), F32),
                pltpu.VMEM((max(nblk, 2 * QR // NBLK), half, NBLK), F32),
                pltpu.VMEM((2 * nblk, half, NBLK), BF16),
                dma((2, KCH)), dma((KCH,)), dma((KCH,)), dma((QR // NBLK,)), dma((RING, 2)), dma((ngrp, 2)), dma((WO_SLOTS,)),
                dma((6,)), dma((8,)), dma((2,)), dma((2,)), dma((2,)), dma((2,)), dma((2, ngrp)), dma((2, ngrp)),
                dma((2 * nblk,)), dma((2 * nblk,)), dma((2 * nblk,)), dma((2 * nblk,)), dma((2 * nblk,)),
            ],
            compiler_params=pltpu.CompilerParams(collective_id=0, has_side_effects=True,
                                                 vmem_limit_bytes=65536 * 1000),
        )(tok_x, tok_pos.reshape(2, half), w_dq, g_q.reshape(QR // 128, 128), w_uq, w_qr, w_dkv, g_kv.reshape(LR // 128, 128), w_kr.T,
          w_uk, w_uv, w_o)

    return jax.shard_map(local_step, mesh=mesh,
                         in_specs=(tok_spec, pos_spec, full_mat, full_vec, col_spec, col_spec, full_mat, full_vec, full_mat, col_spec, col_spec, row_spec),
                         out_specs=tok_spec, check_vma=False)
```

time: 152 us -> 138 us (0.908)
  Pallas kernels: 145 us -> 134 us
  local copies, waits for them, and re-layouts: 6.42 us -> 3.88 us
    pallas_call x1, Pallas kernels: 145 us -> 134 us  [local_step(): pl.pallas_call(functools.partial(layer_kernel, dims), out_shape=jax.Shape...]
    reshape x2 -> x0, local copies, waits for them, and re-layouts: 2.54 us -> none  [the longest x1 1.28 us: local_step(): g_q.reshape(1, QR)]
where the time goes in v2:
time: 138 us; the launch traced here: 137 us
  Pallas kernels  134 us (97%)
  local copies, waits for them, and re-layouts  3.88 us (3%)
    pallas_call x1, Pallas kernels, local_step(): pl.pallas_call(functools.partial(layer_kernel, dims), out_shape=jax.Shape...  134 us
    unnamed x1, local copies, waits for them, and re-layouts  3.88 us

profile of v2, /device:TPU:0, one launch (start us, length us, event | category | flops | bytes accessed | tf_op | source)
XLA Modules:
  0.0 137.5 jit_solution(7757719583233100562)
XLA Ops:
  0.0 133.6 %shard_map.118 = bf16[256,6144]{1,0:T(8,128)(2,1)} custom-call(bf16[256,6144]{1,0:T(8,128)(2,1)} %x_hbm.1, s32[2,128]{1,0:T(2,128)} %bitcast.6, bf16[6144,1536]{1,0:T(8,128)(2,1)} %wdq_hbm.1, bf16[12,128]{1,0:T(8,128)(2,1)} %bitcast.5, bf16[1536,4096]{1,0:T(8,128)(2,1)} %wuq_hbm.1, bf16[1536,2048]{1,0:T(8,128)(2,1)} %wqr_hbm.1, bf16[6144,512]{1,0:T(8,128)(2,1)} %wdkv_hbm.1, ...), custom_call_target="tpu_custom_call" | custom-call | tf_op jit(solution)/shard_map/pallas_call | solution.py:477
  133.6 3.9 %copy.14 = bf16[256,6144]{1,0:T(8,128)(2,1)} copy(bf16[256,6144]{1,0:T(8,128)(2,1)} %shard_map.118) | data formatting | bytes 6291456

commit v3 on v2

--- a/solution.py
+++ b/solution.py
@@ -17,7 +17,9 @@
 KCH = 6
 NBLK = 256
 RING = 3
-WO_SLOTS = 9
+DQ_SLOTS = 4
+GROUP = 4
+WO_SLOTS = 6
 
 
 def _dot(a, b):
@@ -29,10 +31,10 @@
 
 
 def layer_kernel(dims, x_hbm, pos_ref, wdq_hbm, gq_ref, wuq_hbm, wqr_hbm, wdkv_hbm, gkv_ref, wkr_hbm, wuk_hbm, wuv_hbm,
-                 wo_hbm, y_hbm,
+                 wo_hbm, y_ref,
                  xv, kvs, wkr, upw, arena, lat, kplo, kphi, cq, acckv, acckr, rot,
-                 uqb, qrb, qn, qp, os, orx, sendb, recvb, ownb, resb,
-                 xsem, kvsem, krsem, bsem, qsem, upsem, wosem, lats, latr, cqs, cqr, rots, rotr, oss, osr, ps, pr, rs, rr, ys):
+                 uqb, qrb, qn, qp, os, orx, sendb, recvb, ownb,
+                 xsem, x2sem, kvsem, krsem, bsem, qsem, upsem, wosem, lats, latr, cqs, cqr, rots, rotr, oss, osr, ps, pr, rs, rr):
     D, QR, LR, HL, half, score_scale = dims
     HC = HL // 2
     ngrp = HC // 4
@@ -53,10 +55,13 @@
     first_pos = (2 * half * lax.div(ci, 2), half * (6 - 2 * lax.div(ci, 2)))
     half_rows = (slice(0, half), slice(half, 2 * half))
 
-    def x_copy(hf, k):
-        col = pl.multiple_of(k * kc, 128)
-        rows = pl.ds(hf * half, half)
-        return pltpu.make_async_copy(x_hbm.at[rows, pl.ds(col, kc)], xv.at[rows, pl.ds(col, kc)], xsem.at[hf, k])
+    def x_copy(k):
+        rows, cols = pl.ds(0, half), pl.ds(pl.multiple_of(k * kc, 128), kc)
+        return pltpu.make_async_copy(x_hbm.at[rows, cols], xv.at[rows, cols], xsem.at[k])
+
+    def x2_copy():
+        rows = pl.ds(half, half)
+        return pltpu.make_async_copy(x_hbm.at[rows, :], xv.at[rows, :], x2sem.at[0])
 
     def a_copies(k):
         col = pl.multiple_of(k * kc, 128)
@@ -64,8 +69,9 @@
                 pltpu.make_async_copy(wdkv_hbm.at[pl.ds(col, kc), :], kvs.at[pl.ds(col, kc), :], kvsem.at[k]))
 
     def b_copy(n):
+        s = lax.rem(n, DQ_SLOTS)
         return pltpu.make_async_copy(wdq_hbm.at[:, pl.ds(pl.multiple_of(n * NBLK, NBLK), NBLK)],
-                                     arena.at[pl.ds(pl.multiple_of(n * D, D), D), :], bsem.at[n])
+                                     arena.at[pl.ds(pl.multiple_of(s * D, D), D), :], bsem.at[s])
 
     def q_copies(g):
         i = lax.rem(g, ngrp) + core * ngrp
@@ -97,10 +103,9 @@
             c.wait()
 
     for k in range(KCH):
-        x_copy(0, k).start()
+        x_copy(k).start()
         start(a_copies(k))
-    for k in range(KCH):
-        x_copy(1, k).start()
+    x2_copy().start()
 
     bar = pltpu.get_barrier_semaphore()
     for dev in ({"tp": 1 - tp}, {"ctx": xpeer}, {"ctx": dpeer}):
@@ -230,7 +235,7 @@
     def o_send(chunk, i):
         cols = pl.ds(pl.multiple_of(i * 512, 512), 512)
         return pltpu.make_async_remote_copy(src_ref=os.at[chunk, theirs[chunk], cols], dst_ref=orx.at[chunk, :, cols],
-                                            send_sem=oss.at[chunk, i], recv_sem=osr.at[chunk, i],
+                                            send_sem=oss.at[chunk], recv_sem=osr.at[chunk],
                                             device_id={"ctx": dpeer}, device_id_type=MESH)
 
     def attention(chunk, nk):
@@ -238,8 +243,12 @@
 
         def body(i, carry):
             if chunk == 0:
-                wo_copy(2 * i).start()
-                wo_copy(2 * i + 1).start()
+                wo_copy(i).start()
+
+                @pl.when(i == ngrp - 1)
+                def _():
+                    for extra in range(ngrp, WO_SLOTS - 1):
+                        wo_copy(extra).start()
             vis = (lax.broadcasted_iota(jnp.int32, (nq, nk), 1)
                    <= lax.broadcasted_iota(jnp.int32, (nq, nk), 0) + first_pos[chunk])
 
@@ -268,11 +277,10 @@
 
         lax.fori_loop(0, ngrp, body, 0)
 
-        def arrive(i, carry):
-            o_send(chunk, i).wait_recv()
-            return carry
-
-        lax.fori_loop(0, ngrp, arrive, 0)
+    def o_all(chunk):
+        return pltpu.make_async_remote_copy(src_ref=os.at[chunk, theirs[chunk], :], dst_ref=orx.at[chunk],
+                                            send_sem=oss.at[chunk], recv_sem=osr.at[chunk],
+                                            device_id={"ctx": dpeer}, device_id_type=MESH)
 
     total_wo = 3 * nblk
     ahead = WO_SLOTS - 1
@@ -280,52 +288,77 @@
 
     def wo_next(L):
         wo_copy(L).wait()
-
+        wo_refill(L)
+
+    def wo_refill(L):
         @pl.when(L + ahead < total_wo)
         def _():
             wo_copy(L + ahead).start()
 
-    def project(chunk, L):
-        base = lax.rem(L, WO_SLOTS) * hv
-        w_here = arena[pl.ds(pl.multiple_of(base + core * hc, hc), hc), :]
-        w_there = arena[pl.ds(pl.multiple_of(base + (1 - core) * hc, hc), hc), :]
-        return _dot(os[chunk, mine[chunk], :], w_here) + _dot(orx[chunk], w_there)
-
-    def part_send(t):
-        return pltpu.make_async_remote_copy(src_ref=sendb.at[lax.rem(t, nblk)], dst_ref=recvb.at[t], send_sem=ps.at[t],
-                                            recv_sem=pr.at[t],
+    def project_here(chunk, L):
+        w = arena[pl.ds(pl.multiple_of(lax.rem(L, WO_SLOTS) * hv + core * hc, hc), hc), :]
+        return _dot(os[chunk, mine[chunk], :], w)
+
+    def project_there(chunk, L):
+        w = arena[pl.ds(pl.multiple_of(lax.rem(L, WO_SLOTS) * hv + (1 - core) * hc, hc), hc), :]
+        return _dot(orx[chunk], w)
+
+    def part_copy(chunk, q, src, dst):
+        return pltpu.make_async_remote_copy(src_ref=src, dst_ref=dst, send_sem=ps.at[chunk, q], recv_sem=pr.at[chunk, q],
                                             device_id={"tp": 1 - tp}, device_id_type=MESH)
 
+    def part_send(chunk, j):
+        return part_copy(chunk, lax.div(j, GROUP), sendb.at[j], recvb.at[chunk * nblk + j])
+
+    def part_group(chunk, q):
+        return part_copy(chunk, q, sendb.at[pl.ds(q * GROUP, GROUP)], recvb.at[pl.ds(chunk * nblk + q * GROUP, GROUP)])
+
     def project_partner(chunk):
+        early = 2
+        base = chunk * nblk
+
+        def send_slot(j):
+            if chunk == 1:
+                @pl.when(lax.rem(j, GROUP) == 0)
+                def _():
+                    part_group(0, lax.div(j, GROUP)).wait_send()
+
+        for j in range(early):
+            wo_copy(base + j).wait()
+            if j == 0:
+                wo_refill(base)
+            send_slot(j)
+            sendb[j] = project_here(chunk, base + j)
+        o_all(chunk).wait_recv()
+        for j in range(early):
+            sendb[j] += project_there(chunk, base + j)
+            part_send(chunk, j).start()
+            if j + 1 < early:
+                wo_refill(base + j + 1)
+
         def body(j, carry):
-            t = chunk * nblk + j
-            wo_next(t)
-            if chunk == 1:
-                part_send(j).wait_send()
-            sendb[j] = project(chunk, t)
-            part_send(t).start()
+            wo_next(base + j)
+            send_slot(j)
+            sendb[j] = project_here(chunk, base + j) + project_there(chunk, base + j)
+            part_send(chunk, j).start()
             return carry
 
-        lax.fori_loop(0, nblk, body, 0)
-
-    def y_block(chunk, j, side):
-        return y_hbm.at[pl.ds(chunk * half, half), pl.ds(pl.multiple_of(side * own_cols + j * NBLK, NBLK), NBLK)]
-
-    def result_send(chunk, j, side):
-        t = chunk * nblk + j
-        return pltpu.make_async_remote_copy(src_ref=resb.at[t], dst_ref=y_block(chunk, j, side), send_sem=rs.at[t],
-                                            recv_sem=rr.at[t], device_id={"tp": 1 - tp}, device_id_type=MESH)
-
-    def result_store(chunk, j):
-        t = chunk * nblk + j
-        return pltpu.make_async_copy(resb.at[t], y_block(chunk, j, tp), ys.at[t])
+        lax.fori_loop(early, nblk, body, 0)
+
+    def y_cols(side, j, n):
+        return pl.ds(pl.multiple_of(side * own_cols + j * NBLK, NBLK), n)
+
+    def result_copy(ref):
+        return pltpu.make_async_remote_copy(src_ref=ref, dst_ref=ref, send_sem=rs.at[0], recv_sem=rr.at[0],
+                                            device_id={"tp": 1 - tp}, device_id_type=MESH)
 
     def give_back(chunk, j, own):
-        t = chunk * nblk + j
-        part_send(t).wait_recv()
-        resb[t] = (recvb[t] + own).astype(BF16)
-        result_send(chunk, j, tp).start()
-        result_store(chunk, j).start()
+        @pl.when(lax.rem(j, GROUP) == 0)
+        def _():
+            part_group(chunk, lax.div(j, GROUP)).wait_recv()
+        cols = y_cols(tp, j, NBLK)
+        y_ref[half_rows[chunk], cols] = (recvb[chunk * nblk + j] + own).astype(BF16)
+        result_copy(y_ref.at[half_rows[chunk], cols]).start()
 
     acckv[...] = jnp.zeros_like(acckv)
     acckr[...] = jnp.zeros_like(acckr)
@@ -333,7 +366,7 @@
         rotary(0)
 
     def a_step(k, carry):
-        x_copy(0, k).wait()
+        x_copy(k).wait()
         wait(a_copies(k))
 
         @pl.when(k % 2 == 1)
@@ -354,8 +387,7 @@
     with jax.named_scope('rot1'):
         rotary(1)
         rot_send(1).start()
-        for k in range(KCH):
-            x_copy(1, k).wait()
+        x2_copy().wait()
 
     def b_step(n, carry):
         b_copy(n).wait()
@@ -371,7 +403,7 @@
         @pl.when(n >= nb_q - RING)
         def _():
             start(q_copies(n - (nb_q - RING)))
-        w = arena[pl.ds(pl.multiple_of(n * D, D), D), :]
+        w = arena[pl.ds(pl.multiple_of(lax.rem(n, DQ_SLOTS) * D, D), D), :]
         r = _dot(xv[...], w)
         ownb[n] = r[:half]
         ownb[nb_q + n] = r[half:]
@@ -418,8 +450,8 @@
     def own_body(j, carry):
         L = 2 * nblk + j
         wo_next(L)
-        ownb[j] = project(1, L)
-        give_back(0, j, project(0, L))
+        ownb[j] = project_here(1, L) + project_there(1, L)
+        give_back(0, j, project_here(0, L) + project_there(0, L))
         return carry
 
     with jax.named_scope('own'):
@@ -432,23 +464,17 @@
     with jax.named_scope('ret'):
         lax.fori_loop(0, nblk, ret_body, 0)
 
-    def drain(j, carry):
-        part_send(nblk + j).wait_send()
-        for chunk in range(2):
-            result_send(chunk, j, tp).wait_send()
-            result_store(chunk, j).wait()
-            result_send(chunk, j, 1 - tp).wait_recv()
-        return carry
-
     with jax.named_scope('drain'):
-        lax.fori_loop(0, nblk, drain, 0)
+        for q in range(nblk // GROUP):
+            part_group(1, q).wait_send()
+        result_copy(y_ref.at[:, y_cols(tp, 0, own_cols)]).wait_send()
+        result_copy(y_ref.at[:, y_cols(1 - tp, 0, own_cols)]).wait_recv()
     for slot, piece in ((0, pieces[0]), (1, pieces[0]), (2, pieces[1]), (3, pieces[1]), (4, far[0]), (5, far[1])):
         lat_send(piece, slot, dpeer).wait_send()
     for hf in range(2):
         rot_send(hf).wait_send()
         cq_send(hf).wait_send()
-        for i in range(ngrp):
-            o_send(hf, i).wait_send()
+        o_all(hf).wait_send()
 
 
 def solution(mesh):
@@ -473,12 +499,12 @@
         anyspec = pl.BlockSpec(memory_space=pl.ANY)
         vspec = pl.BlockSpec(memory_space=pltpu.VMEM)
         dma = pltpu.SemaphoreType.DMA
-        arena_rows = max(QR // NBLK * D, WO_SLOTS * HL * 128)
+        arena_rows = max(DQ_SLOTS * D, WO_SLOTS * HL * 128)
         return pl.pallas_call(
             functools.partial(layer_kernel, dims),
-            out_shape=jax.ShapeDtypeStruct((rows, D), BF16),
+            out_shape=pltpu.VMEM((rows, D), BF16),
             in_specs=[anyspec, vspec, anyspec, vspec, anyspec, anyspec, anyspec, vspec, anyspec, anyspec, anyspec, anyspec],
-            out_specs=anyspec,
+            out_specs=vspec,
             scratch_shapes=[
                 pltpu.VMEM((rows, D), BF16),
                 pltpu.VMEM((max(D, 2 * ngrp * ntok), LR), BF16),
@@ -501,13 +527,12 @@
                 pltpu.VMEM((nblk, half, NBLK), F32),
                 pltpu.VMEM((2 * nblk, half, NBLK), F32),
                 pltpu.VMEM((max(nblk, 2 * QR // NBLK), half, NBLK), F32),
-                pltpu.VMEM((2 * nblk, half, NBLK), BF16),
-                dma((2, KCH)), dma((KCH,)), dma((KCH,)), dma((QR // NBLK,)), dma((RING, 2)), dma((ngrp, 2)), dma((WO_SLOTS,)),
-                dma((6,)), dma((8,)), dma((2,)), dma((2,)), dma((2,)), dma((2,)), dma((2, ngrp)), dma((2, ngrp)),
-                dma((2 * nblk,)), dma((2 * nblk,)), dma((2 * nblk,)), dma((2 * nblk,)), dma((2 * nblk,)),
+                dma((KCH,)), dma((1,)), dma((KCH,)), dma((KCH,)), dma((DQ_SLOTS,)), dma((RING, 2)), dma((ngrp, 2)), dma((WO_SLOTS,)),
+                dma((6,)), dma((8,)), dma((2,)), dma((2,)), dma((2,)), dma((2,)), dma((2,)), dma((2,)),
+                dma((2, nblk // GROUP)), dma((2, nblk // GROUP)), dma((1,)), dma((1,)),
             ],
             compiler_params=pltpu.CompilerParams(collective_id=0, has_side_effects=True,
-                                                 vmem_limit_bytes=65536 * 1000),
+                                                 vmem_limit_bytes=60500 * 1000),
         )(tok_x, tok_pos.reshape(2, half), w_dq, g_q.reshape(QR // 128, 128), w_uq, w_qr, w_dkv, g_kv.reshape(LR // 128, 128), w_kr.T,
           w_uk, w_uv, w_o)
 

time: 138 us -> 134 us (0.971)
  local copies, waits for them, and re-layouts: 3.88 us -> 1.67 us
  Pallas kernels: 134 us -> 132 us
    unnamed x1, local copies, waits for them, and re-layouts: 3.88 us -> 1.67 us
where the time goes in v3:
time: 134 us
  Pallas kernels  132 us (99%)
  local copies, waits for them, and re-layouts  1.67 us (1%)
    pallas_call x1, Pallas kernels, local_step(): pl.pallas_call(functools.partial(layer_kernel, dims), out_shape=pltpu.VME...  132 us

profile of v3, /device:TPU:0, one launch (start us, length us, event | category | flops | bytes accessed | tf_op | source)
XLA Modules:
  0.0 134.1 jit_solution(10412708243095672488)
XLA Ops:
  0.0 132.4 %shard_map.118 = bf16[256,6144]{1,0:T(8,128)(2,1)S(1)} custom-call(bf16[256,6144]{1,0:T(8,128)(2,1)} %x_hbm.1, s32[2,128]{1,0:T(2,128)} %bitcast.6, bf16[6144,1536]{1,0:T(8,128)(2,1)} %wdq_hbm.1, bf16[12,128]{1,0:T(8,128)(2,1)} %bitcast.5, bf16[1536,4096]{1,0:T(8,128)(2,1)} %wuq_hbm.1, bf16[1536,2048]{1,0:T(8,128)(2,1)} %wqr_hbm.1, ...), custom_call_target="tpu_custom_call" | custom-call | tf_op jit(solution)/shard_map/pallas_call | solution.py:503
  132.4 1.7 %copy.14 = bf16[256,6144]{1,0:T(8,128)(2,1)} copy(bf16[256,6144]{1,0:T(8,128)(2,1)S(1)} %shard_map.118) | data formatting | bytes 6291456

commit v4 on v3

--- a/solution.py
+++ b/solution.py
@@ -32,9 +32,9 @@
 
 def layer_kernel(dims, x_hbm, pos_ref, wdq_hbm, gq_ref, wuq_hbm, wqr_hbm, wdkv_hbm, gkv_ref, wkr_hbm, wuk_hbm, wuv_hbm,
                  wo_hbm, y_ref,
-                 xv, kvs, wkr, upw, arena, lat, kplo, kphi, cq, acckv, acckr, rot,
+                 xc, x2, kvs, wkr, upw, arena, lat, kplo, kphi, cq, acckv, acckr, rot,
                  uqb, qrb, qn, qp, os, orx, sendb, recvb, ownb,
-                 xsem, x2sem, kvsem, krsem, bsem, qsem, upsem, wosem, lats, latr, cqs, cqr, rots, rotr, oss, osr, ps, pr, rs, rr):
+                 xsem, x2sem, xps, xpr, kvsem, krsem, bsem, qsem, upsem, wosem, lats, latr, cqs, cqr, hs, hr, rots, rotr, oss, osr, ps, pr, rs, rr):
     D, QR, LR, HL, half, score_scale = dims
     HC = HL // 2
     ngrp = HC // 4
@@ -56,20 +56,23 @@
     half_rows = (slice(0, half), slice(half, 2 * half))
 
     def x_copy(k):
-        rows, cols = pl.ds(0, half), pl.ds(pl.multiple_of(k * kc, 128), kc)
-        return pltpu.make_async_copy(x_hbm.at[rows, cols], xv.at[rows, cols], xsem.at[k])
+        cols = pl.ds(pl.multiple_of(k * kc, 128), kc)
+        return pltpu.make_async_copy(x_hbm.at[pl.ds(0, half), cols], xc.at[mine[0], cols], xsem.at[k])
 
     def x2_copy():
-        rows = pl.ds(half, half)
-        return pltpu.make_async_copy(x_hbm.at[rows, :], xv.at[rows, :], x2sem.at[0])
+        return pltpu.make_async_copy(x_hbm.at[pl.ds(half, half), :], x2, x2sem.at[0])
+
+    def x_share(rows):
+        return pltpu.make_async_remote_copy(src_ref=x_hbm.at[pl.ds(0, half), :], dst_ref=xc.at[rows, :], send_sem=xps.at[0],
+                                            recv_sem=xpr.at[0], device_id={"ctx": dpeer}, device_id_type=MESH)
 
     def a_copies(k):
         col = pl.multiple_of(k * kc, 128)
         return (pltpu.make_async_copy(wkr_hbm.at[:, pl.ds(col, kc)], wkr.at[:, pl.ds(col, kc)], krsem.at[k]),
                 pltpu.make_async_copy(wdkv_hbm.at[pl.ds(col, kc), :], kvs.at[pl.ds(col, kc), :], kvsem.at[k]))
 
-    def b_copy(n):
-        s = lax.rem(n, DQ_SLOTS)
+    def b_copy(m, n):
+        s = lax.rem(m, DQ_SLOTS)
         return pltpu.make_async_copy(wdq_hbm.at[:, pl.ds(pl.multiple_of(n * NBLK, NBLK), NBLK)],
                                      arena.at[pl.ds(pl.multiple_of(s * D, D), D), :], bsem.at[s])
 
@@ -105,7 +108,6 @@
     for k in range(KCH):
         x_copy(k).start()
         start(a_copies(k))
-    x2_copy().start()
 
     bar = pltpu.get_barrier_semaphore()
     for dev in ({"tp": 1 - tp}, {"ctx": xpeer}, {"ctx": dpeer}):
@@ -179,27 +181,34 @@
         kplo[rows, :] = jnp.where(low, kp, 0.0).astype(BF16)
         kphi[rows, :] = jnp.where(low, 0.0, kp).astype(BF16)
 
-    def qlat_finish(hf):
+    nb_c = nb_q // 2
+
+    def half_send(m):
+        ref = ownb.at[pl.ds(2 * (core * nb_c + m), 2)]
+        return to_core(ref, hs.at[0], hr.at[0])
+
+    def half_all(side):
+        ref = ownb.at[pl.ds(2 * side * nb_c, 2 * nb_c)]
+        return to_core(ref, hs.at[0], hr.at[0])
+
+    def norm_queries(chunk, rows, block):
         sq = 0.0
         for n in range(nb_q):
-            a = ownb[hf * nb_q + n]
+            a = ownb[block(n)]
             sq = sq + jnp.sum(a * a, axis=-1, keepdims=True)
         inv = lax.rsqrt(sq * (1.0 / QR) + NORM_EPS)
         for n in range(nb_q):
-            a = ownb[hf * nb_q + n] * inv
+            a = ownb[block(n)] * inv
             for u in range(NBLK // 128):
                 c = n * (NBLK // 128) + u
-                cq[hf, mine[hf], c * 128:(c + 1) * 128] = (
+                cq[chunk, rows, c * 128:(c + 1) * 128] = (
                     a[:, u * 128:(u + 1) * 128] * gq_ref[c:c + 1, :].astype(F32)).astype(BF16)
 
-    def cq_send(hf):
-        return to_core(cq.at[hf, mine[hf], :], cqs.at[hf], cqr.at[hf])
-
-    def cq_recv(hf):
-        return to_core(cq.at[hf, theirs[hf], :], cqs.at[hf], cqr.at[hf])
+    def cq_share(rows):
+        return to_core(cq.at[1, rows, :], cqs.at[0], cqr.at[0])
 
     def queries(chunk):
-        def body(i, carry):
+        def group(i):
             g = i + chunk * ngrp
             s = lax.rem(g, RING)
             wait(q_copies(g))
@@ -212,6 +221,13 @@
             @pl.when(g + RING < 2 * ngrp)
             def _():
                 start(q_copies(g + RING))
+
+        def body(i, carry):
+            if chunk == 0:
+                @pl.when(i == ngrp // 2)
+                def _():
+                    forward(0)
+            group(i)
             return carry
 
         lax.fori_loop(0, ngrp, body, 0)
@@ -220,15 +236,20 @@
         return pl.ds(pl.multiple_of(i * ntok, ntok), n)
 
     def keys_values(chunk, nk):
-        def body(i, carry):
+        per = 2 if chunk == 0 else 1
+
+        def body(t, carry):
             if chunk == 0:
-                wait(up_copies(i))
+                for u in range(per):
+                    wait(up_copies(per * t + u))
             lt = lat[0:nk, 0:LR]
-            kvs[kv_rows(i, nk), :] = _dot(lt, upw[i]).astype(BF16)
-            kvs[kv_rows(ngrp + i, nk), :] = _dot(lt, upw[ngrp + i]).astype(BF16)
+            for u in range(per):
+                i = per * t + u
+                kvs[kv_rows(i, nk), :] = _dot(lt, upw[i]).astype(BF16)
+                kvs[kv_rows(ngrp + i, nk), :] = _dot(lt, upw[ngrp + i]).astype(BF16)
             return carry
 
-        lax.fori_loop(0, ngrp, body, 0)
+        lax.fori_loop(0, ngrp // per, body, 0)
 
     c2e = score_scale * 1.4426950408889634
 
@@ -242,13 +263,12 @@
         nq = 2 * half
 
         def body(i, carry):
-            if chunk == 0:
-                wo_copy(i).start()
-
-                @pl.when(i == ngrp - 1)
-                def _():
-                    for extra in range(ngrp, WO_SLOTS - 1):
-                        wo_copy(extra).start()
+            wo_copy(chunk * nblk + i).start()
+
+            @pl.when(i == ngrp - 1)
+            def _():
+                for extra in range(ngrp, WO_SLOTS - 1):
+                    wo_copy(chunk * nblk + extra).start()
             vis = (lax.broadcasted_iota(jnp.int32, (nq, nk), 1)
                    <= lax.broadcasted_iota(jnp.int32, (nq, nk), 0) + first_pos[chunk])
 
@@ -291,7 +311,7 @@
         wo_refill(L)
 
     def wo_refill(L):
-        @pl.when(L + ahead < total_wo)
+        @pl.when(jnp.logical_and(L + ahead < total_wo, jnp.logical_or(L >= nblk, L + ahead < nblk)))
         def _():
             wo_copy(L + ahead).start()
 
@@ -365,81 +385,96 @@
     with jax.named_scope('rot0'):
         rotary(0)
 
+    pl.semaphore_wait(bar, 3)
+    x_share(mine[0]).start()
+
     def a_step(k, carry):
         x_copy(k).wait()
         wait(a_copies(k))
 
-        @pl.when(k % 2 == 1)
+        @pl.when(lax.rem(k, 2) == 0)
         def _():
-            b_copy(lax.div(k, 2)).start()
+            m = lax.div(k, 2)
+            b_copy(m, core * nb_c + m).start()
         cols = pl.ds(pl.multiple_of(k * kc, 128), kc)
-        xk = xv[half_rows[0], cols]
+        xk = xc[mine[0], cols]
         acckv[...] += _dot(xk, kvs[cols, :])
         acckr[...] += _dot_nt(xk, wkr[:, cols])
         return carry
 
     with jax.named_scope('lat0'):
         lax.fori_loop(0, KCH, a_step, 0)
+        x2_copy().start()
         lat_finish(0, acckv[...], acckr[...])
-        pl.semaphore_wait(bar, 3)
         lat_share(0)
         rot_send(0).start()
-    with jax.named_scope('rot1'):
+    with jax.named_scope('xwait'):
+        x_share(theirs[0]).wait_recv()
+
+    def dq_block(m, rows):
+        return _dot(rows, arena[pl.ds(pl.multiple_of(lax.rem(m, DQ_SLOTS) * D, D), D), :])
+
+    def b_step(m, carry):
+        n = core * nb_c + m
+        b_copy(m, n).wait()
+        start(q_copies(m))
+        r = dq_block(m, xc[...])
+        ownb[2 * n] = r[:half]
+        ownb[2 * n + 1] = r[half:]
+        half_send(m).start()
+        return carry
+
+    with jax.named_scope('qlat0'):
+        lax.fori_loop(0, nb_c, b_step, 0)
+        for m in range(nb_c, RING):
+            start(q_copies(m))
+        for i in range(ngrp):
+            start(up_copies(i))
+    with jax.named_scope('lat1'):
         rotary(1)
         rot_send(1).start()
         x2_copy().wait()
-
-    def b_step(n, carry):
-        b_copy(n).wait()
-
-        @pl.when(n < nb_q - 3)
-        def _():
-            b_copy(n + 3).start()
-
-        @pl.when(n < ngrp)
-        def _():
-            start(up_copies(n))
-
-        @pl.when(n >= nb_q - RING)
-        def _():
-            start(q_copies(n - (nb_q - RING)))
-        w = arena[pl.ds(pl.multiple_of(lax.rem(n, DQ_SLOTS) * D, D), D), :]
-        r = _dot(xv[...], w)
-        ownb[n] = r[:half]
-        ownb[nb_q + n] = r[half:]
-        return carry
-
-    with jax.named_scope('qlat'):
-        lax.fori_loop(0, nb_q, b_step, 0)
-    with jax.named_scope('qfin'):
-        forward(0)
-        qlat_finish(0)
-        cq_send(0).start()
-    with jax.named_scope('lat1'):
-        xs = xv[half_rows[1], :]
+        xs = x2[...]
         lat_finish(1, _dot(xs, kvs[0:D, :]), _dot_nt(xs, wkr[...]))
         lat_share(1)
-        qlat_finish(1)
-        cq_send(1).start()
+    with jax.named_scope('qfin0'):
+        half_all(1 - core).wait_recv()
+        for sl in range(2):
+            norm_queries(0, half_rows[sl], lambda n, sl=sl: 2 * n + sl)
+        rot_recv(0).wait_recv()
+    with jax.named_scope('q0'):
+        queries(0)
     with jax.named_scope('gather0'):
         gathered(0)
     with jax.named_scope('kv0'):
         keys_values(0, 4 * half)
-    with jax.named_scope('q0'):
-        cq_recv(0).wait_recv()
-        rot_recv(0).wait_recv()
-        queries(0)
     with jax.named_scope('att0'):
         attention(0, 4 * half)
     with jax.named_scope('part0'):
         project_partner(0)
+
+    def b1_step(n, carry):
+        @pl.when(n + 3 < nb_q)
+        def _():
+            b_copy(n + 3, n + 3).start()
+        b_copy(n, n).wait()
+        ownb[n] = dq_block(n, x2[...])
+        return carry
+
+    with jax.named_scope('qlat1'):
+        half_all(core).wait_send()
+        for n in range(3):
+            b_copy(n, n).start()
+        forward(1)
+        lax.fori_loop(0, nb_q, b1_step, 0)
+        norm_queries(1, mine[1], lambda n: n)
+        cq_share(mine[1]).start()
     with jax.named_scope('gather1'):
-        forward(1)
         gathered(1)
     with jax.named_scope('kv1'):
         keys_values(1, 8 * half)
     with jax.named_scope('q1'):
-        cq_recv(1).wait_recv()
+        cq_share(theirs[1]).wait_recv()
         rot_recv(1).wait_recv()
         queries(1)
     with jax.named_scope('att1'):
@@ -471,9 +506,10 @@
         result_copy(y_ref.at[:, y_cols(1 - tp, 0, own_cols)]).wait_recv()
     for slot, piece in ((0, pieces[0]), (1, pieces[0]), (2, pieces[1]), (3, pieces[1]), (4, far[0]), (5, far[1])):
         lat_send(piece, slot, dpeer).wait_send()
+    x_share(mine[0]).wait_send()
+    cq_share(mine[1]).wait_send()
     for hf in range(2):
         rot_send(hf).wait_send()
-        cq_send(hf).wait_send()
         o_all(hf).wait_send()
 
 
@@ -507,6 +543,7 @@
             out_specs=vspec,
             scratch_shapes=[
                 pltpu.VMEM((rows, D), BF16),
+                pltpu.VMEM((half, D), BF16),
                 pltpu.VMEM((max(D, 2 * ngrp * ntok), LR), BF16),
                 pltpu.VMEM((64, D), BF16),
                 pltpu.VMEM((2 * ngrp, LR, 512), BF16),
@@ -527,8 +564,8 @@
                 pltpu.VMEM((nblk, half, NBLK), F32),
                 pltpu.VMEM((2 * nblk, half, NBLK), F32),
                 pltpu.VMEM((max(nblk, 2 * QR // NBLK), half, NBLK), F32),
-                dma((KCH,)), dma((1,)), dma((KCH,)), dma((KCH,)), dma((DQ_SLOTS,)), dma((RING, 2)), dma((ngrp, 2)), dma((WO_SLOTS,)),
-                dma((6,)), dma((8,)), dma((2,)), dma((2,)), dma((2,)), dma((2,)), dma((2,)), dma((2,)),
+                dma((KCH,)), dma((1,)), dma((1,)), dma((1,)), dma((KCH,)), dma((KCH,)), dma((DQ_SLOTS,)), dma((RING, 2)), dma((ngrp, 2)), dma((WO_SLOTS,)),
+                dma((6,)), dma((8,)), dma((1,)), dma((1,)), dma((1,)), dma((1,)), dma((2,)), dma((2,)), dma((2,)), dma((2,)),
                 dma((2, nblk // GROUP)), dma((2, nblk // GROUP)), dma((1,)), dma((1,)),
             ],
             compiler_params=pltpu.CompilerParams(collective_id=0, has_side_effects=True,

time: 134 us -> 130 us (0.970)
  Pallas kernels: 132 us -> 129 us
    pallas_call x1, Pallas kernels: 132 us -> 129 us  [local_step(): pl.pallas_call(functools.partial(layer_kernel, dims), out_shape=pltpu.VME...]
where the time goes in v4:
time: 130 us
  Pallas kernels  129 us (99%)
  local copies, waits for them, and re-layouts  1.67 us (1%)
    pallas_call x1, Pallas kernels, local_step(): pl.pallas_call(functools.partial(layer_kernel, dims), out_shape=pltpu.VME...  129 us

profile of v4, /device:TPU:0, one launch (start us, length us, event | category | flops | bytes accessed | tf_op | source)
XLA Modules:
  0.0 130.3 jit_solution(9992579103198174170)
XLA Ops:
  0.0 128.6 %shard_map.118 = bf16[256,6144]{1,0:T(8,128)(2,1)S(1)} custom-call(bf16[256,6144]{1,0:T(8,128)(2,1)} %x_hbm.1, s32[2,128]{1,0:T(2,128)} %bitcast.6, bf16[6144,1536]{1,0:T(8,128)(2,1)} %wdq_hbm.1, bf16[12,128]{1,0:T(8,128)(2,1)} %bitcast.5, bf16[1536,4096]{1,0:T(8,128)(2,1)} %wuq_hbm.1, bf16[1536,2048]{1,0:T(8,128)(2,1)} %wqr_hbm.1, ...), custom_call_target="tpu_custom_call" | custom-call | tf_op jit(solution)/shard_map/pallas_call | solution.py:539
  128.7 1.7 %copy.14 = bf16[256,6144]{1,0:T(8,128)(2,1)} copy(bf16[256,6144]{1,0:T(8,128)(2,1)S(1)} %shard_map.118) | data formatting | bytes 6291456

commit v5 on v4

--- a/solution.py
+++ b/solution.py
@@ -16,7 +16,7 @@
 
 KCH = 6
 NBLK = 256
-RING = 3
+RING = 4
 DQ_SLOTS = 4
 GROUP = 4
 WO_SLOTS = 6
@@ -30,11 +30,11 @@
     return lax.dot_general(a, b, (((1,), (1,)), ((), ())), preferred_element_type=F32)
 
 
-def layer_kernel(dims, x_hbm, pos_ref, wdq_hbm, gq_ref, wuq_hbm, wqr_hbm, wdkv_hbm, gkv_ref, wkr_hbm, wuk_hbm, wuv_hbm,
+def layer_kernel(dims, x_hbm, pos_hbm, wdq_hbm, gq_hbm, wuq_hbm, wqr_hbm, wdkv_hbm, gkv_hbm, wkr_hbm, wuk_hbm, wuv_hbm,
                  wo_hbm, y_ref,
-                 xc, x2, kvs, wkr, upw, arena, lat, kplo, kphi, cq, acckv, acckr, rot,
+                 pos_ref, gq_ref, gkv_ref, xc, x2, kvs, wkr, upw, arena, lat, kplo, kphi, cq, acckv, acckr, rot,
                  uqb, qrb, qn, qp, os, orx, sendb, recvb, ownb,
-                 xsem, x2sem, xps, xpr, kvsem, krsem, bsem, qsem, upsem, wosem, lats, latr, cqs, cqr, hs, hr, rots, rotr, oss, osr, ps, pr, rs, rr):
+                 smsem, xsem, x2sem, xps, xpr, kvsem, krsem, bsem, qsem, upsem, wosem, lats, latr, cqs, cqr, hs, hr, rots, rotr, oss, osr, ps, pr, rs, rr):
     D, QR, LR, HL, half, score_scale = dims
     HC = HL // 2
     ngrp = HC // 4
@@ -105,13 +105,16 @@
         for c in cps:
             c.wait()
 
+    bar = pltpu.get_barrier_semaphore()
+    for dev in ({"ctx": xpeer}, {"tp": 1 - tp}, {"ctx": dpeer}):
+        pl.semaphore_signal(bar, inc=1, device_id=dev, device_id_type=MESH)
+
+    small = (pltpu.make_async_copy(pos_hbm, pos_ref, smsem.at[0]), pltpu.make_async_copy(gkv_hbm, gkv_ref, smsem.at[1]),
+             pltpu.make_async_copy(gq_hbm, gq_ref, smsem.at[2]))
+    start(small)
     for k in range(KCH):
         x_copy(k).start()
         start(a_copies(k))
-
-    bar = pltpu.get_barrier_semaphore()
-    for dev in ({"tp": 1 - tp}, {"ctx": xpeer}, {"ctx": dpeer}):
-        pl.semaphore_signal(bar, inc=1, device_id=dev, device_id_type=MESH)
 
     lane = lax.broadcasted_iota(jnp.int32, (1, 128), 1)
     first_half = lax.rem(lane, 64) < 32
@@ -208,29 +211,30 @@
         return to_core(cq.at[1, rows, :], cqs.at[0], cqr.at[0])
 
     def queries(chunk):
-        def group(i):
-            g = i + chunk * ngrp
-            s = lax.rem(g, RING)
-            wait(q_copies(g))
-            c = cq[chunk]
-            r = _dot(c, qrb[s])
-            qn[:, pl.ds(pl.multiple_of(i * 512, 512), 512)] = _dot(c, uqb[s]).astype(BF16)
-            for u in range(2):
-                qp[:, pl.ds(pl.multiple_of(i * 256 + u * 128, 128), 128)] = turn(r[:, u * 128:(u + 1) * 128], rot[chunk]).astype(BF16)
-
-            @pl.when(g + RING < 2 * ngrp)
-            def _():
-                start(q_copies(g + RING))
-
-        def body(i, carry):
+        def body(t, carry):
             if chunk == 0:
-                @pl.when(i == ngrp // 2)
+                @pl.when(t == 1)
                 def _():
                     forward(0)
-            group(i)
+            gs = [2 * t + u + chunk * ngrp for u in range(2)]
+            for g in gs:
+                wait(q_copies(g))
+            c = cq[chunk]
+            for u in range(2):
+                i = 2 * t + u
+                s = lax.rem(gs[u], RING)
+                r = _dot(c, qrb[s])
+                qn[:, pl.ds(pl.multiple_of(i * 512, 512), 512)] = _dot(c, uqb[s]).astype(BF16)
+                for v in range(2):
+                    qp[:, pl.ds(pl.multiple_of(i * 256 + v * 128, 128), 128)] = turn(
+                        r[:, v * 128:(v + 1) * 128], rot[chunk]).astype(BF16)
+            for g in gs:
+                @pl.when(g + RING < 2 * ngrp)
+                def _():
+                    start(q_copies(g + RING))
             return carry
 
-        lax.fori_loop(0, ngrp, body, 0)
+        lax.fori_loop(0, ngrp // 2, body, 0)
 
     def kv_rows(i, n):
         return pl.ds(pl.multiple_of(i * ntok, ntok), n)
@@ -378,19 +382,25 @@
             part_group(chunk, lax.div(j, GROUP)).wait_recv()
         cols = y_cols(tp, j, NBLK)
         y_ref[half_rows[chunk], cols] = (recvb[chunk * nblk + j] + own).astype(BF16)
-        result_copy(y_ref.at[half_rows[chunk], cols]).start()
+
+        @pl.when(lax.rem(j, GROUP) == GROUP - 1)
+        def _():
+            result_copy(y_ref.at[half_rows[chunk], y_cols(tp, j - (GROUP - 1), GROUP * NBLK)]).start()
 
     acckv[...] = jnp.zeros_like(acckv)
     acckr[...] = jnp.zeros_like(acckr)
-    with jax.named_scope('rot0'):
-        rotary(0)
-
-    pl.semaphore_wait(bar, 3)
-    x_share(mine[0]).start()
-
     def a_step(k, carry):
+        @pl.when(k == 1)
+        def _():
+            pl.semaphore_wait(bar, 3)
+            x_share(mine[0]).start()
         x_copy(k).wait()
         wait(a_copies(k))
+
+        @pl.when(k == 3)
+        def _():
+            wait(small)
+            rotary(0)
 
         @pl.when(lax.rem(k, 2) == 0)
         def _():
@@ -539,9 +549,12 @@
         return pl.pallas_call(
             functools.partial(layer_kernel, dims),
             out_shape=pltpu.VMEM((rows, D), BF16),
-            in_specs=[anyspec, vspec, anyspec, vspec, anyspec, anyspec, anyspec, vspec, anyspec, anyspec, anyspec, anyspec],
+            in_specs=[anyspec, anyspec, anyspec, anyspec, anyspec, anyspec, anyspec, anyspec, anyspec, anyspec, anyspec, anyspec],
             out_specs=vspec,
             scratch_shapes=[
+                pltpu.VMEM((2, half), jnp.int32),
+                pltpu.VMEM((QR // 128, 128), BF16),
+                pltpu.VMEM((LR // 128, 128), BF16),
                 pltpu.VMEM((rows, D), BF16),
                 pltpu.VMEM((half, D), BF16),
                 pltpu.VMEM((max(D, 2 * ngrp * ntok), LR), BF16),
@@ -564,12 +577,12 @@
                 pltpu.VMEM((nblk, half, NBLK), F32),
                 pltpu.VMEM((2 * nblk, half, NBLK), F32),
                 pltpu.VMEM((max(nblk, 2 * QR // NBLK), half, NBLK), F32),
-                dma((KCH,)), dma((1,)), dma((1,)), dma((1,)), dma((KCH,)), dma((KCH,)), dma((DQ_SLOTS,)), dma((RING, 2)), dma((ngrp, 2)), dma((WO_SLOTS,)),
+                dma((3,)), dma((KCH,)), dma((1,)), dma((1,)), dma((1,)), dma((KCH,)), dma((KCH,)), dma((DQ_SLOTS,)), dma((RING, 2)), dma((ngrp, 2)), dma((WO_SLOTS,)),
                 dma((6,)), dma((8,)), dma((1,)), dma((1,)), dma((1,)), dma((1,)), dma((2,)), dma((2,)), dma((2,)), dma((2,)),
                 dma((2, nblk // GROUP)), dma((2, nblk // GROUP)), dma((1,)), dma((1,)),
             ],
             compiler_params=pltpu.CompilerParams(collective_id=0, has_side_effects=True,
-                                                 vmem_limit_bytes=60500 * 1000),
+                                                 vmem_limit_bytes=62500 * 1000),
         )(tok_x, tok_pos.reshape(2, half), w_dq, g_q.reshape(QR // 128, 128), w_uq, w_qr, w_dkv, g_kv.reshape(LR // 128, 128), w_kr.T,
           w_uk, w_uv, w_o)
 

time: 130 us -> 130 us (level)
  no operation moved by 1% of the time
where the time goes in v5:
time: 130 us
  Pallas kernels  128 us (98%)
  local copies, waits for them, and re-layouts  1.67 us (1%)
    pallas_call x1, Pallas kernels, local_step(): pl.pallas_call(functools.partial(layer_kernel, dims), out_shape=pltpu.VME...  128 us

profile of v5, /device:TPU:0, one launch (start us, length us, event | category | flops | bytes accessed | tf_op | source)
XLA Modules:
  0.0 129.7 jit_solution(3695999431675558135)
XLA Ops:
  0.0 128.0 %shard_map.118 = bf16[256,6144]{1,0:T(8,128)(2,1)S(1)} custom-call(bf16[256,6144]{1,0:T(8,128)(2,1)} %x_hbm.1, s32[2,128]{1,0:T(2,128)} %bitcast.6, bf16[6144,1536]{1,0:T(8,128)(2,1)} %wdq_hbm.1, bf16[12,128]{1,0:T(8,128)(2,1)} %bitcast.5, bf16[1536,4096]{1,0:T(8,128)(2,1)} %wuq_hbm.1, bf16[1536,2048]{1,0:T(8,128)(2,1)} %wqr_hbm.1, ...), custom_call_target="tpu_custom_call" | custom-call | tf_op jit(solution)/shard_map/pallas_call | solution.py:549
  128.0 1.7 %copy.14 = bf16[256,6144]{1,0:T(8,128)(2,1)} copy(bf16[256,6144]{1,0:T(8,128)(2,1)S(1)} %shard_map.118) | data formatting | bytes 6291456

commit v6 on v5

--- a/solution.py
+++ b/solution.py
@@ -50,6 +50,7 @@
     xpeer = lax.rem(ci + 2, 4)
     dpeer = ci + 1 - 2 * core
     pieces = (ci, 7 - ci)
+    pair = lax.div(ci, 2)
     mine = tuple(pl.ds(pl.multiple_of(sl * half, half), half) for sl in (core, 1 - core))
     theirs = tuple(pl.ds(pl.multiple_of(sl * half, half), half) for sl in (1 - core, core))
     first_pos = (2 * half * lax.div(ci, 2), half * (6 - 2 * lax.div(ci, 2)))
@@ -175,10 +176,8 @@
         lat_recv(far[hf])
         lat_send(far[hf], 4 + hf, dpeer).start()
 
-    def gathered(hf):
-        lat_recv(near[hf])
-        lat_recv(relayed[hf])
-        rows = slice(hf * 4 * half, (hf + 1) * 4 * half)
+    def split_rope(lo, hi):
+        rows = slice(lo, hi)
         kp = lat[rows, LR:LR + 128].astype(F32)
         low = lane < 64
         kplo[rows, :] = jnp.where(low, kp, 0.0).astype(BF16)
@@ -213,7 +212,7 @@
     def queries(chunk):
         def body(t, carry):
             if chunk == 0:
-                @pl.when(t == 1)
+                @pl.when(jnp.logical_and(t == 1, pair == 1))
                 def _():
                     forward(0)
             gs = [2 * t + u + chunk * ngrp for u in range(2)]
@@ -263,7 +262,7 @@
                                             send_sem=oss.at[chunk], recv_sem=osr.at[chunk],
                                             device_id={"ctx": dpeer}, device_id_type=MESH)
 
-    def attention(chunk, nk):
+    def attention(chunk, nk, clear):
         nq = 2 * half
 
         def body(i, carry):
@@ -273,8 +272,8 @@
             def _():
                 for extra in range(ngrp, WO_SLOTS - 1):
                     wo_copy(chunk * nblk + extra).start()
-            vis = (lax.broadcasted_iota(jnp.int32, (nq, nk), 1)
-                   <= lax.broadcasted_iota(jnp.int32, (nq, nk), 0) + first_pos[chunk])
+            vis = (lax.broadcasted_iota(jnp.int32, (nq, nk - clear), 1)
+                   <= lax.broadcasted_iota(jnp.int32, (nq, nk - clear), 0) + (first_pos[chunk] - clear))
 
             def scores(h):
                 kp = kphi if h % 2 else kplo
@@ -284,7 +283,8 @@
                 return _dot_nt(qh, kh)
 
             def values(h, sc):
-                sc = jnp.where(vis, sc, NEG_BIG)
+                late = jnp.where(vis, sc[:, clear:], NEG_BIG)
+                sc = jnp.concatenate([sc[:, :clear], late], axis=1) if clear else late
                 top = jnp.max(sc, axis=1, keepdims=True)
                 p = jnp.exp2((sc - top) * c2e)
                 tot = jnp.sum(p, axis=1, keepdims=True)
@@ -390,10 +390,6 @@
     acckv[...] = jnp.zeros_like(acckv)
     acckr[...] = jnp.zeros_like(acckr)
     def a_step(k, carry):
-        @pl.when(k == 1)
-        def _():
-            pl.semaphore_wait(bar, 3)
-            x_share(mine[0]).start()
         x_copy(k).wait()
         wait(a_copies(k))
 
@@ -402,16 +398,23 @@
             wait(small)
             rotary(0)
 
-        @pl.when(lax.rem(k, 2) == 0)
-        def _():
-            m = lax.div(k, 2)
+        @pl.when(jnp.logical_and(lax.rem(k, 2) == 0, k < 2 * nb_c - 2))
+        def _():
+            m = lax.div(k, 2) + 1
             b_copy(m, core * nb_c + m).start()
+
+        @pl.when(k == KCH - 1)
+        def _():
+            start(q_copies(0))
         cols = pl.ds(pl.multiple_of(k * kc, 128), kc)
         xk = xc[mine[0], cols]
         acckv[...] += _dot(xk, kvs[cols, :])
         acckr[...] += _dot_nt(xk, wkr[:, cols])
         return carry
 
+    b_copy(0, core * nb_c).start()
+    pl.semaphore_wait(bar, 3)
+    x_share(mine[0]).start()
     with jax.named_scope('lat0'):
         lax.fori_loop(0, KCH, a_step, 0)
         x2_copy().start()
@@ -427,7 +430,7 @@
     def b_step(m, carry):
         n = core * nb_c + m
         b_copy(m, n).wait()
-        start(q_copies(m))
+        start(q_copies(m + 1))
         r = dq_block(m, xc[...])
         ownb[2 * n] = r[:half]
         ownb[2 * n + 1] = r[half:]
@@ -436,17 +439,13 @@
 
     with jax.named_scope('qlat0'):
         lax.fori_loop(0, nb_c, b_step, 0)
-        for m in range(nb_c, RING):
+        for m in range(nb_c + 1, RING):
             start(q_copies(m))
         for i in range(ngrp):
             start(up_copies(i))
     with jax.named_scope('lat1'):
-        rotary(1)
-        rot_send(1).start()
         x2_copy().wait()
-        xs = x2[...]
-        lat_finish(1, _dot(xs, kvs[0:D, :]), _dot_nt(xs, wkr[...]))
-        lat_share(1)
+        acckv[...] = _dot(x2[...], kvs[0:D, :])
     with jax.named_scope('qfin0'):
         half_all(1 - core).wait_recv()
         for sl in range(2):
@@ -454,12 +453,19 @@
         rot_recv(0).wait_recv()
     with jax.named_scope('q0'):
         queries(0)
-    with jax.named_scope('gather0'):
-        gathered(0)
-    with jax.named_scope('kv0'):
-        keys_values(0, 4 * half)
-    with jax.named_scope('att0'):
-        attention(0, 4 * half)
+    for which in range(2):
+        @pl.when(pair == which)
+        def _():
+            nk = 2 * half * (which + 1)
+            with jax.named_scope('gather0'):
+                lat_recv(near[0])
+                if which == 1:
+                    lat_recv(relayed[0])
+                split_rope(0, nk)
+            with jax.named_scope('kv0'):
+                keys_values(0, nk)
+            with jax.named_scope('att0'):
+                attention(0, nk, nk - 2 * half)
     with jax.named_scope('part0'):
         project_partner(0)
 
@@ -475,12 +481,24 @@
         half_all(core).wait_send()
         for n in range(3):
             b_copy(n, n).start()
-        forward(1)
+        rotary(1)
+        rot_send(1).start()
+        lat_finish(1, acckv[...], _dot_nt(x2[...], wkr[...]))
+        lat_share(1)
         lax.fori_loop(0, nb_q, b1_step, 0)
         norm_queries(1, mine[1], lambda n: n)
         cq_share(mine[1]).start()
     with jax.named_scope('gather1'):
-        gathered(1)
+        forward(1)
+
+        @pl.when(pair == 0)
+        def _():
+            forward(0)
+            lat_recv(relayed[0])
+            split_rope(2 * half, 4 * half)
+        lat_recv(near[1])
+        lat_recv(relayed[1])
+        split_rope(4 * half, 8 * half)
     with jax.named_scope('kv1'):
         keys_values(1, 8 * half)
     with jax.named_scope('q1'):
@@ -488,7 +506,7 @@
         rot_recv(1).wait_recv()
         queries(1)
     with jax.named_scope('att1'):
-        attention(1, 8 * half)
+        attention(1, 8 * half, 4 * half)
     with jax.named_scope('part1'):
         project_partner(1)
 

time: 130 us -> 127 us (0.977)
  Pallas kernels: 128 us -> 125 us
    pallas_call x1, Pallas kernels: 128 us -> 125 us  [local_step(): pl.pallas_call(functools.partial(layer_kernel, dims), out_shape=pltpu.VME...]
where the time goes in v6:
time: 127 us; the launch traced here: 126 us
  Pallas kernels  125 us (98%)
  local copies, waits for them, and re-layouts  1.67 us (1%)
    pallas_call x1, Pallas kernels, local_step(): pl.pallas_call(functools.partial(layer_kernel, dims), out_shape=pltpu.VME...  125 us

profile of v6, /device:TPU:0, one launch (start us, length us, event | category | flops | bytes accessed | tf_op | source)
XLA Modules:
  0.0 126.2 jit_solution(14220459743626804254)
XLA Ops:
  0.0 124.5 %shard_map.118 = bf16[256,6144]{1,0:T(8,128)(2,1)S(1)} custom-call(bf16[256,6144]{1,0:T(8,128)(2,1)} %x_hbm.1, s32[2,128]{1,0:T(2,128)} %bitcast.6, bf16[6144,1536]{1,0:T(8,128)(2,1)} %wdq_hbm.1, bf16[12,128]{1,0:T(8,128)(2,1)} %bitcast.5, bf16[1536,4096]{1,0:T(8,128)(2,1)} %wuq_hbm.1, bf16[1536,2048]{1,0:T(8,128)(2,1)} %wqr_hbm.1, ...), custom_call_target="tpu_custom_call" | custom-call | tf_op jit(solution)/shard_map/pallas_call | solution.py:567
  124.5 1.7 %copy.14 = bf16[256,6144]{1,0:T(8,128)(2,1)} copy(bf16[256,6144]{1,0:T(8,128)(2,1)S(1)} %shard_map.118) | data formatting | bytes 6291456

commit v7 on v6

--- a/solution.py
+++ b/solution.py
@@ -19,6 +19,7 @@
 RING = 4
 DQ_SLOTS = 4
 GROUP = 4
+UNROLL = 4
 WO_SLOTS = 6
 
 
@@ -239,7 +240,7 @@
         return pl.ds(pl.multiple_of(i * ntok, ntok), n)
 
     def keys_values(chunk, nk):
-        per = 2 if chunk == 0 else 1
+        per = ngrp if chunk == 0 else 1
 
         def body(t, carry):
             if chunk == 0:
@@ -265,41 +266,46 @@
     def attention(chunk, nk, clear):
         nq = 2 * half
 
-        def body(i, carry):
-            wo_copy(chunk * nblk + i).start()
-
-            @pl.when(i == ngrp - 1)
+        vis = (lax.broadcasted_iota(jnp.int32, (nq, nk - clear), 1)
+               <= lax.broadcasted_iota(jnp.int32, (nq, nk - clear), 0) + (first_pos[chunk] - clear))
+
+        def scores(i, h):
+            kp = kphi if h % 2 else kplo
+            qpe = qp[:, pl.ds(pl.multiple_of(i * 256 + (h // 2) * 128, 128), 128)]
+            qh = jnp.concatenate([qn[:, pl.ds(pl.multiple_of(i * 512 + h * 128, 128), 128)], qpe], axis=1)
+            kh = jnp.concatenate([kvs[kv_rows(i, nk), h * 128:(h + 1) * 128], kp[0:nk, :]], axis=1)
+            return _dot_nt(qh, kh)
+
+        def values(i, h, sc):
+            late = jnp.where(vis, sc[:, clear:], NEG_BIG)
+            sc = jnp.concatenate([sc[:, :clear], late], axis=1) if clear else late
+            top = jnp.max(sc, axis=1, keepdims=True)
+            p = jnp.exp2((sc - top) * c2e)
+            tot = jnp.sum(p, axis=1, keepdims=True)
+            acc = _dot(p.astype(BF16), kvs[kv_rows(ngrp + i, nk), h * 128:(h + 1) * 128])
+            os[chunk, :, pl.ds(pl.multiple_of(i * 512 + h * 128, 128), 128)] = (acc / tot).astype(BF16)
+
+        per = UNROLL if chunk == 0 else 1
+
+        def body(t, carry):
+            for u in range(per):
+                wo_copy(chunk * nblk + per * t + u).start()
+
+            @pl.when(t == ngrp // per - 1)
             def _():
                 for extra in range(ngrp, WO_SLOTS - 1):
                     wo_copy(chunk * nblk + extra).start()
-            vis = (lax.broadcasted_iota(jnp.int32, (nq, nk - clear), 1)
-                   <= lax.broadcasted_iota(jnp.int32, (nq, nk - clear), 0) + (first_pos[chunk] - clear))
-
-            def scores(h):
-                kp = kphi if h % 2 else kplo
-                qpe = qp[:, pl.ds(pl.multiple_of(i * 256 + (h // 2) * 128, 128), 128)]
-                qh = jnp.concatenate([qn[:, pl.ds(pl.multiple_of(i * 512 + h * 128, 128), 128)], qpe], axis=1)
-                kh = jnp.concatenate([kvs[kv_rows(i, nk), h * 128:(h + 1) * 128], kp[0:nk, :]], axis=1)
-                return _dot_nt(qh, kh)
-
-            def values(h, sc):
-                late = jnp.where(vis, sc[:, clear:], NEG_BIG)
-                sc = jnp.concatenate([sc[:, :clear], late], axis=1) if clear else late
-                top = jnp.max(sc, axis=1, keepdims=True)
-                p = jnp.exp2((sc - top) * c2e)
-                tot = jnp.sum(p, axis=1, keepdims=True)
-                acc = _dot(p.astype(BF16), kvs[kv_rows(ngrp + i, nk), h * 128:(h + 1) * 128])
-                os[chunk, :, pl.ds(pl.multiple_of(i * 512 + h * 128, 128), 128)] = (acc / tot).astype(BF16)
-
-            sc = scores(0)
-            for h in range(4):
-                nxt = scores(h + 1) if h < 3 else None
-                values(h, sc)
+            sc = scores(per * t, 0)
+            for u in range(4 * per):
+                i, h = per * t + u // 4, u % 4
+                nxt = scores(per * t + (u + 1) // 4, (u + 1) % 4) if u + 1 < 4 * per else None
+                values(i, h, sc)
                 sc = nxt
-            o_send(chunk, i).start()
+                if h == 3:
+                    o_send(chunk, i).start()
             return carry
 
-        lax.fori_loop(0, ngrp, body, 0)
+        lax.fori_loop(0, ngrp // per, body, 0)
 
     def o_all(chunk):
         return pltpu.make_async_remote_copy(src_ref=os.at[chunk, theirs[chunk], :], dst_ref=orx.at[chunk],

time: 127 us -> 126 us (level)
  no operation moved by 1% of the time
where the time goes in v7:
time: 126 us
  Pallas kernels  124 us (98%)
  local copies, waits for them, and re-layouts  1.67 us (1%)
    pallas_call x1, Pallas kernels, local_step(): pl.pallas_call(functools.partial(layer_kernel, dims), out_shape=pltpu.VME...  124 us

profile of v7, /device:TPU:0, one launch (start us, length us, event | category | flops | bytes accessed | tf_op | source)
XLA Modules:
  0.0 125.7 jit_solution(15110503165006219346)
XLA Ops:
  0.0 124.0 %shard_map.118 = bf16[256,6144]{1,0:T(8,128)(2,1)S(1)} custom-call(bf16[256,6144]{1,0:T(8,128)(2,1)} %x_hbm.1, s32[2,128]{1,0:T(2,128)} %bitcast.6, bf16[6144,1536]{1,0:T(8,128)(2,1)} %wdq_hbm.1, bf16[12,128]{1,0:T(8,128)(2,1)} %bitcast.5, bf16[1536,4096]{1,0:T(8,128)(2,1)} %wuq_hbm.1, bf16[1536,2048]{1,0:T(8,128)(2,1)} %wqr_hbm.1, ...), custom_call_target="tpu_custom_call" | custom-call | tf_op jit(solution)/shard_map/pallas_call | solution.py:573
  124.0 1.7 %copy.14 = bf16[256,6144]{1,0:T(8,128)(2,1)} copy(bf16[256,6144]{1,0:T(8,128)(2,1)S(1)} %shard_map.118) | data formatting | bytes 6291456

commit v8 on v7

--- a/solution.py
+++ b/solution.py
@@ -9,7 +9,7 @@
 
 ROPE_BASE = 10000.0
 NORM_EPS = 1e-6
-NEG_BIG = -1e30
+NEG_BIG = float("-inf")
 MESH = pl.DeviceIdType.MESH
 F32 = jnp.float32
 BF16 = jnp.bfloat16
@@ -20,6 +20,7 @@
 DQ_SLOTS = 4
 GROUP = 4
 UNROLL = 4
+KV_PIECES = ((0,), (1,), (2, 3), ())
 WO_SLOTS = 6
 
 
@@ -35,7 +36,7 @@
                  wo_hbm, y_ref,
                  pos_ref, gq_ref, gkv_ref, xc, x2, kvs, wkr, upw, arena, lat, kplo, kphi, cq, acckv, acckr, rot,
                  uqb, qrb, qn, qp, os, orx, sendb, recvb, ownb,
-                 smsem, xsem, x2sem, xps, xpr, kvsem, krsem, bsem, qsem, upsem, wosem, lats, latr, cqs, cqr, hs, hr, rots, rotr, oss, osr, ps, pr, rs, rr):
+                 smsem, xsem, x2sem, xps, xpr, kvsem, krsem, qsem, upsem, wosem, lats, latr, cqs, cqr, hs, hr, rots, rotr, oss, osr, ps, pr, rs, rr):
     D, QR, LR, HL, half, score_scale = dims
     HC = HL // 2
     ngrp = HC // 4
@@ -76,7 +77,7 @@
     def b_copy(m, n):
         s = lax.rem(m, DQ_SLOTS)
         return pltpu.make_async_copy(wdq_hbm.at[:, pl.ds(pl.multiple_of(n * NBLK, NBLK), NBLK)],
-                                     arena.at[pl.ds(pl.multiple_of(s * D, D), D), :], bsem.at[s])
+                                     arena.at[pl.ds(pl.multiple_of(s * D, D), D), :], wosem.at[s])
 
     def q_copies(g):
         i = lax.rem(g, ngrp) + core * ngrp
@@ -148,9 +149,9 @@
     def rot_recv(hf):
         return to_core(rot.at[hf, theirs[hf], :], rots.at[hf], rotr.at[hf])
 
-    def lat_send(piece, slot, dev):
+    def lat_send(piece, dev):
         ref = lat.at[pl.ds(pl.multiple_of(piece * half, half), half), :]
-        return pltpu.make_async_remote_copy(src_ref=ref, dst_ref=ref, send_sem=lats.at[slot], recv_sem=latr.at[piece],
+        return pltpu.make_async_remote_copy(src_ref=ref, dst_ref=ref, send_sem=lats.at[0], recv_sem=latr.at[piece],
                                             device_id={"ctx": dev}, device_id_type=MESH)
 
     def lat_finish(hf, a, kr):
@@ -163,19 +164,19 @@
         lat[pl.ds(row0, half), LR:LR + 128] = kr2.astype(BF16)
 
     def lat_share(hf):
-        lat_send(pieces[hf], 2 * hf, xpeer).start()
-        lat_send(pieces[hf], 2 * hf + 1, dpeer).start()
+        lat_send(pieces[hf], xpeer).start()
+        lat_send(pieces[hf], dpeer).start()
 
     far = (xpeer, 7 - xpeer)
     near = (dpeer, 7 - dpeer)
     relayed = (3 - ci, 4 + ci)
 
     def lat_recv(piece):
-        lat_send(piece, 0, dpeer).wait_recv()
+        lat_send(piece, dpeer).wait_recv()
 
     def forward(hf):
         lat_recv(far[hf])
-        lat_send(far[hf], 4 + hf, dpeer).start()
+        lat_send(far[hf], dpeer).start()
 
     def split_rope(lo, hi):
         rows = slice(lo, hi)
@@ -237,23 +238,30 @@
         lax.fori_loop(0, ngrp // 2, body, 0)
 
     def kv_rows(i, n):
+        if isinstance(i, int):
+            return slice(i * ntok, i * ntok + n)
         return pl.ds(pl.multiple_of(i * ntok, ntok), n)
 
+    def kv_part(i, quarter, nk):
+        m = i + ngrp * (quarter // 2)
+        cols = slice(256 * (quarter % 2), 256 * (quarter % 2) + 256)
+        kvs[m * ntok:m * ntok + nk, cols] = _dot(lat[0:nk, 0:LR], upw[m, :, cols]).astype(BF16)
+
     def keys_values(chunk, nk):
-        per = ngrp if chunk == 0 else 1
-
-        def body(t, carry):
-            if chunk == 0:
-                for u in range(per):
-                    wait(up_copies(per * t + u))
+        if chunk == 0:
+            for i in range(ngrp):
+                wait(up_copies(i))
+            for quarter in range(4):
+                kv_part(0, quarter, nk)
+            return
+
+        def body(i, carry):
             lt = lat[0:nk, 0:LR]
-            for u in range(per):
-                i = per * t + u
-                kvs[kv_rows(i, nk), :] = _dot(lt, upw[i]).astype(BF16)
-                kvs[kv_rows(ngrp + i, nk), :] = _dot(lt, upw[ngrp + i]).astype(BF16)
+            kvs[kv_rows(i, nk), :] = _dot(lt, upw[i]).astype(BF16)
+            kvs[kv_rows(ngrp + i, nk), :] = _dot(lt, upw[ngrp + i]).astype(BF16)
             return carry
 
-        lax.fori_loop(0, ngrp // per, body, 0)
+        lax.fori_loop(0, ngrp, body, 0)
 
     c2e = score_scale * 1.4426950408889634
 
@@ -291,21 +299,31 @@
             for u in range(per):
                 wo_copy(chunk * nblk + per * t + u).start()
 
-            @pl.when(t == ngrp // per - 1)
-            def _():
+            def rest():
                 for extra in range(ngrp, WO_SLOTS - 1):
                     wo_copy(chunk * nblk + extra).start()
+
+            if per == ngrp:
+                rest()
+            else:
+                pl.when(t == ngrp // per - 1)(rest)
             sc = scores(per * t, 0)
             for u in range(4 * per):
                 i, h = per * t + u // 4, u % 4
                 nxt = scores(per * t + (u + 1) // 4, (u + 1) % 4) if u + 1 < 4 * per else None
+                if per == ngrp and i + 1 < ngrp:
+                    for quarter in KV_PIECES[h]:
+                        kv_part(i + 1, quarter, nk)
                 values(i, h, sc)
                 sc = nxt
                 if h == 3:
                     o_send(chunk, i).start()
             return carry
 
-        lax.fori_loop(0, ngrp // per, body, 0)
+        if per == ngrp:
+            body(0, 0)
+        else:
+            lax.fori_loop(0, ngrp // per, body, 0)
 
     def o_all(chunk):
         return pltpu.make_async_remote_copy(src_ref=os.at[chunk, theirs[chunk], :], dst_ref=orx.at[chunk],
@@ -538,8 +556,9 @@
             part_group(1, q).wait_send()
         result_copy(y_ref.at[:, y_cols(tp, 0, own_cols)]).wait_send()
         result_copy(y_ref.at[:, y_cols(1 - tp, 0, own_cols)]).wait_recv()
-    for slot, piece in ((0, pieces[0]), (1, pieces[0]), (2, pieces[1]), (3, pieces[1]), (4, far[0]), (5, far[1])):
-        lat_send(piece, slot, dpeer).wait_send()
+    six = lat.at[pl.ds(0, 6 * half), :]
+    pltpu.make_async_remote_copy(src_ref=six, dst_ref=six, send_sem=lats.at[0], recv_sem=latr.at[0],
+                                 device_id={"ctx": dpeer}, device_id_type=MESH).wait_send()
     x_share(mine[0]).wait_send()
     cq_share(mine[1]).wait_send()
     for hf in range(2):
@@ -601,8 +620,8 @@
                 pltpu.VMEM((nblk, half, NBLK), F32),
                 pltpu.VMEM((2 * nblk, half, NBLK), F32),
                 pltpu.VMEM((max(nblk, 2 * QR // NBLK), half, NBLK), F32),
-                dma((3,)), dma((KCH,)), dma((1,)), dma((1,)), dma((1,)), dma((KCH,)), dma((KCH,)), dma((DQ_SLOTS,)), dma((RING, 2)), dma((ngrp, 2)), dma((WO_SLOTS,)),
-                dma((6,)), dma((8,)), dma((1,)), dma((1,)), dma((1,)), dma((1,)), dma((2,)), dma((2,)), dma((2,)), dma((2,)),
+                dma((3,)), dma((KCH,)), dma((1,)), dma((1,)), dma((1,)), dma((KCH,)), dma((KCH,)), dma((RING, 2)), dma((ngrp, 2)), dma((WO_SLOTS,)),
+                dma((1,)), dma((8,)), dma((1,)), dma((1,)), dma((1,)), dma((1,)), dma((2,)), dma((2,)), dma((2,)), dma((2,)),
                 dma((2, nblk // GROUP)), dma((2, nblk // GROUP)), dma((1,)), dma((1,)),
             ],
             compiler_params=pltpu.CompilerParams(collective_id=0, has_side_effects=True,

time: 126 us -> 126 us (level)
  no operation moved by 1% of the time
where the time goes in v8:
time: 126 us; the launch traced here: 125 us
  Pallas kernels  124 us (98%)
  local copies, waits for them, and re-layouts  1.67 us (1%)
    pallas_call x1, Pallas kernels, local_step(): pl.pallas_call(functools.partial(layer_kernel, dims), out_shape=pltpu.VME...  124 us

profile of v8, /device:TPU:0, one launch (start us, length us, event | category | flops | bytes accessed | tf_op | source)
XLA Modules:
  0.0 125.3 jit_solution(14270091366604084534)
XLA Ops:
  0.0 123.6 %shard_map.118 = bf16[256,6144]{1,0:T(8,128)(2,1)S(1)} custom-call(bf16[256,6144]{1,0:T(8,128)(2,1)} %x_hbm.1, s32[2,128]{1,0:T(2,128)} %bitcast.6, bf16[6144,1536]{1,0:T(8,128)(2,1)} %wdq_hbm.1, bf16[12,128]{1,0:T(8,128)(2,1)} %bitcast.5, bf16[1536,4096]{1,0:T(8,128)(2,1)} %wuq_hbm.1, bf16[1536,2048]{1,0:T(8,128)(2,1)} %wqr_hbm.1, ...), custom_call_target="tpu_custom_call" | custom-call | tf_op jit(solution)/shard_map/pallas_call | solution.py:592
  123.6 1.7 %copy.14 = bf16[256,6144]{1,0:T(8,128)(2,1)} copy(bf16[256,6144]{1,0:T(8,128)(2,1)S(1)} %shard_map.118) | data formatting | bytes 6291456

commit v9 on v8

--- a/solution.py
+++ b/solution.py
@@ -212,17 +212,15 @@
         return to_core(cq.at[1, rows, :], cqs.at[0], cqr.at[0])
 
     def queries(chunk):
+        per = ngrp if chunk == 0 else 2
+
         def body(t, carry):
-            if chunk == 0:
-                @pl.when(jnp.logical_and(t == 1, pair == 1))
-                def _():
-                    forward(0)
-            gs = [2 * t + u + chunk * ngrp for u in range(2)]
+            gs = [per * t + u + chunk * ngrp for u in range(per)]
             for g in gs:
                 wait(q_copies(g))
             c = cq[chunk]
-            for u in range(2):
-                i = 2 * t + u
+            for u in range(per):
+                i = per * t + u
                 s = lax.rem(gs[u], RING)
                 r = _dot(c, qrb[s])
                 qn[:, pl.ds(pl.multiple_of(i * 512, 512), 512)] = _dot(c, uqb[s]).astype(BF16)
@@ -235,7 +233,7 @@
                     start(q_copies(g + RING))
             return carry
 
-        lax.fori_loop(0, ngrp // 2, body, 0)
+        lax.fori_loop(0, ngrp // per, body, 0)
 
     def kv_rows(i, n):
         if isinstance(i, int):
@@ -430,6 +428,7 @@
         @pl.when(k == KCH - 1)
         def _():
             start(q_copies(0))
+            start(q_copies(1))
         cols = pl.ds(pl.multiple_of(k * kc, 128), kc)
         xk = xc[mine[0], cols]
         acckv[...] += _dot(xk, kvs[cols, :])
@@ -454,7 +453,10 @@
     def b_step(m, carry):
         n = core * nb_c + m
         b_copy(m, n).wait()
-        start(q_copies(m + 1))
+
+        @pl.when(m + 2 < RING)
+        def _():
+            start(q_copies(m + 2))
         r = dq_block(m, xc[...])
         ownb[2 * n] = r[:half]
         ownb[2 * n + 1] = r[half:]
@@ -476,6 +478,9 @@
             norm_queries(0, half_rows[sl], lambda n, sl=sl: 2 * n + sl)
         rot_recv(0).wait_recv()
     with jax.named_scope('q0'):
+        @pl.when(pair == 1)
+        def _():
+            forward(0)
         queries(0)
     for which in range(2):
         @pl.when(pair == which)

time: 126 us -> 126 us (level)
  no operation moved by 1% of the time
where the time goes in v9:
time: 126 us
  Pallas kernels  124 us (98%)
  local copies, waits for them, and re-layouts  1.67 us (1%)
    pallas_call x1, Pallas kernels, local_step(): pl.pallas_call(functools.partial(layer_kernel, dims), out_shape=pltpu.VME...  124 us

profile of v9, /device:TPU:0, one launch (start us, length us, event | category | flops | bytes accessed | tf_op | source)
XLA Modules:
  0.0 125.8 jit_solution(16515589458643130062)
XLA Ops:
  0.0 124.1 %shard_map.118 = bf16[256,6144]{1,0:T(8,128)(2,1)S(1)} custom-call(bf16[256,6144]{1,0:T(8,128)(2,1)} %x_hbm.1, s32[2,128]{1,0:T(2,128)} %bitcast.6, bf16[6144,1536]{1,0:T(8,128)(2,1)} %wdq_hbm.1, bf16[12,128]{1,0:T(8,128)(2,1)} %bitcast.5, bf16[1536,4096]{1,0:T(8,128)(2,1)} %wuq_hbm.1, bf16[1536,2048]{1,0:T(8,128)(2,1)} %wqr_hbm.1, ...), custom_call_target="tpu_custom_call" | custom-call | tf_op jit(solution)/shard_map/pallas_call | solution.py:597
  124.2 1.7 %copy.14 = bf16[256,6144]{1,0:T(8,128)(2,1)} copy(bf16[256,6144]{1,0:T(8,128)(2,1)S(1)} %shard_map.118) | data formatting | bytes 6291456
